TPU v7x, 128 devices: a whole 4x4x4 slice. The times are simulated.
128 devices in a mesh: dp: 4 (over y), cp: 32 (over x, z, core).
Axes of the slice: x: 4, y: 4, z: 4, core: 2. Of those that a mesh axis runs over, the one named last changes fastest.
Arguments:
- hidden: bfloat16 [4, 4096, 2880], P('dp', 'cp'), may hold values from -8 to 8
- norm_gain: float32 [2880], replicated, may hold values from 0.5 to 1.5
- query_weight: bfloat16 [2880, 2048], replicated, may hold values from -4 to 4
- keyval_weight: bfloat16 [2880, 512], replicated, may hold values from -1 to 1
- sink_logits: float32 [32], replicated, may hold values from -1 to 3
- document_ids: int32 [4, 4096], P('dp', 'cp'), may hold values from 0 to 15, never falling along the last dimension, each value on 1 to 1024 neighbouring positions
- block_owner: int32 [4, 32, 32], P('dp', 'cp'), may hold values from 0 to 31, each once within a row
- loss_mask: int32 [4, 4096], P('dp', 'cp'), may hold values from 0 to 1, as said below
Outputs:
- attended: bfloat16 [4, 4096, 2048], P('dp', 'cp')
- row_lse: float32 [4, 32, 4096], P('dp', None, 'cp')
- token_weight: float32 [4, 4096], P('dp', 'cp')
Inputs may be any that keep to these rules, and one draw needn't show every extreme that they name: `document_ids`: in each group the ids start at 0, never fall, rise by at most one from a position to the next and end at 15; a document holds at most 1024 positions. `block_owner`: for each group and device the row of 32 entries is a permutation of 0 to 31. `loss_mask`: the last flag of each group is 1.
All inputs are finite; a program needn't handle non-finite values.
Results may differ from a plain program's by a relative error of at most 0.008.
Values may be sent and summed in bfloat16 or wider, within the bound.
A program may use at most 128 MiB of HBM per device.

v0:
```python
import math

import jax
import jax.numpy as jnp
from jax import lax
from jax.sharding import Mesh
from jax.sharding import PartitionSpec as P

HEAD_DIM = 64
CP = ("cp_0", "cp_1", "cp_2")
DP_CP = ("dp", "cp_0", "cp_1", "cp_2")


rope_base = 150000.0
norm_eps = 1e-05
masked_score = -1e30


def by_axis(x, axes):
    for axis in axes:
        x = lax.psum(x, axis)
    return x


def split_up(x, dim, peers):
    dims = x.shape
    blocks = x.reshape(*dims[:dim], peers, dims[dim] // peers, *dims[dim + 1 :])
    return jnp.moveaxis(blocks, dim, 0)


def in_order(blocks, dim):
    blocks = jnp.moveaxis(blocks, 0, dim)
    dims = blocks.shape
    return blocks.reshape(*dims[:dim], dims[dim] * dims[dim + 1], *dims[dim + 2 :])


def turned_blocks(blocks, axes, sequence):
    inside = blocks.shape[1:]
    result = blocks.reshape(*(lax.axis_size(a) for a in axes), *inside)
    for k in sequence:
        result = lax.all_to_all(result, axes[k], k, k, tiled=True)
    return result.reshape(-1, *inside)


def core_and_chips(x, groups, sequence, split_dim, concat_dim):
    peers = lax.axis_size(groups[0]) * lax.axis_size(groups[1])
    blocks = split_up(x, split_dim, peers)
    return in_order(turned_blocks(blocks, groups, sequence), concat_dim)


def rotate(values, within):
    half_dim = values.shape[-1] // 2
    frequency = jnp.power(rope_base, -jnp.arange(half_dim, dtype=jnp.float32) / half_dim)
    angles = within.astype(jnp.float32)[:, None, None] * frequency[None, None, :]
    cosine = jnp.cos(angles)
    sine_part = jnp.sin(angles)
    first = values[..., :half_dim]
    second = values[..., half_dim:]
    return jnp.concatenate(
        [first * cosine - second * sine_part, second * cosine + first * sine_part], axis=-1
    )


def doc_within(doc_index):
    length = doc_index.shape[0]
    places = jnp.arange(length, dtype=jnp.int32)
    fresh_doc = jnp.concatenate([jnp.ones((1,), dtype=bool), doc_index[1:] != doc_index[:-1]])
    starts = lax.cummax(jnp.where(fresh_doc, places, 0), axis=0)
    return places - starts


def plain_places(first_row, key_count):
    return first_row + jnp.arange(key_count, dtype=jnp.int32)


def body(
    hidden,
    norm_gain,
    query_weight,
    keyval_weight,
    sink_logits,
    document_ids,
    block_owner,
    loss_mask,
):
    shards = lax.axis_size(CP)
    my_index = lax.axis_index(CP)
    own_rows = hidden.shape[1]
    block_rows = own_rows // shards
    head_count = sink_logits.shape[0]
    kv_width = keyval_weight.shape[1] // 2
    kv_heads = kv_width // HEAD_DIM
    group_size = head_count // kv_heads
    score_scale = HEAD_DIM ** (-0.5)
    doc_all, owner_all = (
        lax.all_gather(document_ids, CP, axis=1, tiled=True),
        lax.all_gather(block_owner, CP, axis=1, tiled=True),
    )
    doc_index = doc_all[0]
    owner_table = owner_all[0]
    within_all = doc_within(doc_index)
    shard_range = jnp.arange(shards, dtype=jnp.int32)
    inverse = jnp.sum(
        jnp.where(
            owner_table[:, :, None] == shard_range[None, None, :], shard_range[None, :, None], 0
        ),
        axis=1,
    )
    flag_values = loss_mask[0].astype(jnp.float32)
    token_total = by_axis(jnp.sum(flag_values), DP_CP)
    all_tokens = float(lax.axis_size("dp") * shards * own_rows)
    token_weight = (flag_values * (all_tokens / token_total))[None]
    rows_float = hidden[0].astype(jnp.float32)
    inv_rms = lax.rsqrt(jnp.mean(rows_float * rows_float, axis=1, keepdims=True) + norm_eps)
    normed = (rows_float * inv_rms * norm_gain).astype(jnp.bfloat16)
    inner_rows = jnp.tile(jnp.arange(block_rows, dtype=jnp.int32), shards)
    my_blocks = inverse[:, my_index]
    query_place = (
        jnp.repeat(shard_range, block_rows) * own_rows
        + jnp.repeat(my_blocks, block_rows) * block_rows
        + inner_rows
    )
    send_order = inverse[my_index]
    query_place = my_index * own_rows + jnp.arange(own_rows, dtype=jnp.int32)
    own_within = lax.dynamic_slice_in_dim(within_all, my_index * own_rows, own_rows, 0)
    projected = jnp.dot(normed, query_weight, preferred_element_type=jnp.float32).reshape(
        own_rows, head_count, HEAD_DIM
    )
    queries = (
        rotate(projected, own_within).astype(jnp.bfloat16).reshape(own_rows, head_count * HEAD_DIM)
    )
    keyval = jnp.dot(normed, keyval_weight, preferred_element_type=jnp.float32)
    keys_rot = (
        rotate(keyval[:, :kv_width].reshape(own_rows, kv_heads, HEAD_DIM), own_within)
        .astype(jnp.bfloat16)
        .reshape(own_rows, kv_width)
    )
    values = keyval[:, kv_width:].astype(jnp.bfloat16)
    query_doc = doc_index[query_place]
    query_heads = queries.reshape(own_rows, kv_heads, group_size, HEAD_DIM)

    def attend_block(running, key_part, value_part, first_row):
        row_top, row_total, row_sums = running
        key_count = key_part.shape[0]
        places = plain_places(first_row, key_count)
        key_doc = doc_index[places]
        allowed = (query_doc[:, None] == key_doc[None, :]) & (
            places[None, :] <= query_place[:, None]
        )
        scores = jnp.einsum(
            "qagd,kad->agqk",
            query_heads,
            key_part.reshape(key_count, kv_heads, HEAD_DIM),
            preferred_element_type=jnp.float32,
        )
        scores = scores.reshape(head_count, own_rows, key_count) * score_scale
        scores = jnp.where(allowed[None], scores, masked_score)
        new_top = jnp.maximum(row_top, jnp.max(scores, axis=-1))
        exp_scores = jnp.exp(scores - new_top[..., None])
        shrink = jnp.exp(row_top - new_top)
        new_total = row_total * shrink + jnp.sum(exp_scores, axis=-1)
        weights = exp_scores.astype(jnp.bfloat16).reshape(kv_heads, group_size, own_rows, key_count)
        mixed_values = jnp.einsum(
            "agqk,kad->agqd",
            weights,
            value_part.reshape(key_count, kv_heads, HEAD_DIM),
            preferred_element_type=jnp.float32,
        )
        mixed_values = mixed_values.reshape(head_count, own_rows, HEAD_DIM)
        return (new_top, new_total, row_sums * shrink[..., None] + mixed_values)

    initial = (
        jnp.broadcast_to(sink_logits[:, None], (head_count, own_rows)),
        jnp.ones((head_count, own_rows), jnp.float32),
        jnp.zeros((head_count, own_rows, HEAD_DIM), jnp.float32),
    )
    key_piece = lax.all_gather(keys_rot, CP, axis=0, tiled=True)
    value_piece = lax.all_gather(values, CP, axis=0, tiled=True)
    key_count = key_piece.shape[0]
    sub_rows = math.gcd(key_count, max(512, own_rows))

    def one_step(step_index, carried):
        offset = step_index * sub_rows
        key_part = lax.dynamic_slice_in_dim(key_piece, offset, sub_rows, 0)
        value_part = lax.dynamic_slice_in_dim(value_piece, offset, sub_rows, 0)
        return attend_block(carried, key_part, value_part, offset)

    row_top, row_total, row_sums = lax.fori_loop(0, key_count // sub_rows, one_step, initial)
    normalized = (row_sums / row_total[..., None]).astype(jnp.bfloat16)
    normalized = jnp.transpose(normalized, (1, 0, 2)).reshape(
        shards, block_rows, head_count * HEAD_DIM
    )
    log_total = row_top + jnp.log(row_total)
    attended = normalized.reshape(1, own_rows, head_count * HEAD_DIM)
    lse_blocks = jnp.take(log_total.reshape(head_count, shards, block_rows), send_order, axis=1)
    arrived_lse = core_and_chips(lse_blocks, (("cp_0", "cp_1"), "cp_2"), (0, 1), 1, 1)
    row_lse = arrived_lse.reshape(1, head_count, own_rows)
    return (attended, row_lse, token_weight)


def solution(mesh):
    split = Mesh(mesh.devices.reshape(mesh.shape["dp"], 4, 4, 2), ("dp", "cp_0", "cp_1", "cp_2"))
    return jax.shard_map(
        body,
        mesh=split,
        in_specs=(
            P("dp", CP, None),
            P(),
            P(),
            P(),
            P(),
            P("dp", CP),
            P("dp", CP, None),
            P("dp", CP),
        ),
        out_specs=(P("dp", CP, None), P("dp", None, CP), P("dp", CP)),
        check_vma=False,
    )
```

profile of v0, /device:TPU:1, one launch (start us, length us, event | category | flops | bytes accessed | tf_op | source)
XLA Modules:
  0.0 338.6 jit_solution(15831901570877011111)
XLA Ops:
  7.3 24.4 %all_gather.12 = s32[1,4096]{1,0:T(1,128)S(1)} all-gather(s32[1,128]{1,0:T(1,128)} %param.15), channel_id=1, replica_groups=mesh['dp'=4,'cp_0'=4,'cp_1'=4,'cp_2'=2] {'cp_0','cp_1','cp_2'}, dimensions={1}, use_global_device_ids=true | all-gather | bytes 16896 | tf_op jit(solution)/shard_map/all_gather | solution.py:96
  32.5 1.5 fusion.12
  34.1 2.4 fusion.20
  38.2 1.3 convert_reduce_fusion
  39.5 9.3 %psum.28 = f32[]{:T(128)} all-reduce(f32[]{:T(128)} %convert_reduce_fusion), channel_id=1, replica_groups=mesh['dp'=4,'cp_0'=4,'cp_1'=4,'cp_2'=2] {'dp'}, use_global_device_ids=true, to_apply=%region_9.10 | all-reduce | flops 1 | bytes 8 | tf_op jit(solution)/shard_map/psum | solution.py:21
  48.8 8.3 %psum.29 = f32[]{:T(128)} all-reduce(f32[]{:T(128)} %psum.28), channel_id=1, replica_groups=mesh['dp'=4,'cp_0'=4,'cp_1'=4,'cp_2'=2] {'cp_0'}, use_global_device_ids=true, to_apply=%region_10.11 | all-reduce | flops 1 | bytes 8 | tf_op jit(solution)/shard_map/psum | solution.py:21
  57.1 7.3 %psum.30 = f32[]{:T(128)} all-reduce(f32[]{:T(128)} %psum.29), channel_id=1, replica_groups=mesh['dp'=4,'cp_0'=4,'cp_1'=4,'cp_2'=2] {'cp_1'}, use_global_device_ids=true, to_apply=%region_11.12 | all-reduce | flops 1 | bytes 8 | tf_op jit(solution)/shard_map/psum | solution.py:21
  64.4 9.0 %psum.31 = f32[]{:T(128)} all-reduce(f32[]{:T(128)} %psum.30), channel_id=1, replica_groups=mesh['dp'=4,'cp_0'=4,'cp_1'=4,'cp_2'=2] {'cp_2'}, use_global_device_ids=true, to_apply=%region_12.13 | all-reduce | flops 1 | bytes 8 | tf_op jit(solution)/shard_map/psum | solution.py:21
  73.3 16.4 %copy.65 = bf16[2880,2048]{0,1:T(8,128)(2,1)} copy(bf16[2880,2048]{1,0:T(8,128)(2,1)} %param.12) | data formatting | bytes 23592960 | tf_op args[2]
  89.7 1.1 gather_fusion.1
  91.6 20.2 %all_gather.15 = s32[1,32,32]{2,0,1:T(1,128)S(1)} all-gather(s32[1,1,32]{2,0,1:T(1,128)S(1)} %bitcast.142), channel_id=1, replica_groups=mesh['dp'=4,'cp_0'=4,'cp_1'=4,'cp_2'=2] {'cp_0','cp_1','cp_2'}, dimensions={1}, use_global_device_ids=true | all-gather | bytes 4224 | tf_op jit(solution)/shard_map/all_gather | solution.py:97
  112.1 7.2 %fusion.18 = f32[128,32,64]{0,2,1:T(8,128)S(1)} fusion(bf16[32,64,2880]{2,1,0:T(8,128)(2,1)} %bitcast.125, bf16[1,128,2880]{1,2,0:T(8,128)(2,1)} %param.10, f32[2880]{0:T(1024)S(1)} %copy-done.2, f32[128]{0:T(128)S(1)} %add_rsqrt_fusion), kind=kOutput, calls=%fused_computation.37 | convolution fusion | flops 1511424000 | bytes 13594368 | tf_op jit(solution)/shard_map/dot_general | solution.py:126
  120.8 6.5 %all-gather.5.cloned.1.call-done = bf16[4096,256]{1,0:T(8,128)(2,1)} async-done(((bf16[128,256]{1,0:T(8,128)(2,1)}), bf16[4096,256]{1,0:T(8,128)(2,1)}) %all-gather.5.cloned.1.call-update) | async-done | bytes 2097168 | tf_op jit(solution)/shard_map/all_gather | solution.py:178
  127.4 183.6 %while.18 = (s32[]{:T(128)}, f32[32,128]{1,0:T(8,128)S(1)}, f32[32,128]{1,0:T(8,128)S(1)}, f32[32,128,64]{1,2,0:T(8,128)}, s32[128]{0:T(128)S(1)}, /*index=5*/s3...) while((s32[]{:T(128)}, f32[32,128]{1,0:T(8,128)S(1)}, ...), condition=%wide.region_6.7_spmd.clone, body=%wide.region_3.6_spmd.clone.sunk | while | flops 560938624 | bytes 66082540 | solution.py:188
  127.4 1.0 constant_dynamic-slice_fusion.5
  128.4 3.1 gather_fusion
  131.8 5.6 %fusion.46 = (f32[4,8,128]{2,1,0:T(8,128)S(1)}, f32[4,512,128,8]{2,1,3,0:T(8,128)}) fusion(pred[128,512]{0,1:T(8,128)(4,1)S(1)} %compare_and_fusion.3, bf16[512,4,64,1]{0,2,3,1:T(8,128)(2,1)S(1)} %bitcast.126, bf16[128,4,8,64]{0,3,2,1:T(8,128)(2,1)} %get-tuple-element.422), kind=kOutput, calls=%fused_computation.8.clone.1 | convolution fusion | flops 274722816 | bytes 9256960 | tf_op jit(solution)/shard_map/while/body/eval_jaxpr/qagd,kad->agqk/dot_general | solution.py:150
  137.3 1.0 constant_dynamic-slice_fusion.6
  139.1 6.6 %fusion.48 = f32[4,8,128,64]{2,3,1,0:T(8,128)} fusion(bf16[512,4,64,1]{0,2,3,1:T(8,128)(2,1)} %bitcast.129, f32[4,512,128,8]{2,1,3,0:T(8,128)} %get-tuple-element.384, f32[4,8,128]{2,1,0:T(8,128)S(1)} %bitcast.127, pred[128,512]{0,1:T(8,128)(4,1)S(1)} %compare_and_fusion.3), kind=kOutput, calls=%fused_computation.9.clone.1 | convolution fusion | flops 276824064 | bytes 9781248 | tf_op jit(solution)/shard_map/while/body/eval_jaxpr/agqk,kad->agqd/dot_general | solution.py:163
  145.7 1.8 fusion.47
  147.5 2.5 bitcast_add_fusion.5
  150.0 1.0 constant_dynamic-slice_fusion.5
  151.0 3.1 gather_fusion
  154.4 5.6 %fusion.46 = (f32[4,8,128]{2,1,0:T(8,128)S(1)}, f32[4,512,128,8]{2,1,3,0:T(8,128)}) fusion(pred[128,512]{0,1:T(8,128)(4,1)S(1)} %compare_and_fusion.3, bf16[512,4,64,1]{0,2,3,1:T(8,128)(2,1)S(1)} %bitcast.126, bf16[128,4,8,64]{0,3,2,1:T(8,128)(2,1)} %get-tuple-element.422), kind=kOutput, calls=%fused_computation.8.clone.1 | convolution fusion | flops 274722816 | bytes 9256960 | tf_op jit(solution)/shard_map/while/body/eval_jaxpr/qagd,kad->agqk/dot_general | solution.py:150
  160.0 1.0 constant_dynamic-slice_fusion.6
  161.8 6.6 %fusion.48 = f32[4,8,128,64]{2,3,1,0:T(8,128)} fusion(bf16[512,4,64,1]{0,2,3,1:T(8,128)(2,1)} %bitcast.129, f32[4,512,128,8]{2,1,3,0:T(8,128)} %get-tuple-element.384, f32[4,8,128]{2,1,0:T(8,128)S(1)} %bitcast.127, pred[128,512]{0,1:T(8,128)(4,1)S(1)} %compare_and_fusion.3), kind=kOutput, calls=%fused_computation.9.clone.1 | convolution fusion | flops 276824064 | bytes 9781248 | tf_op jit(solution)/shard_map/while/body/eval_jaxpr/agqk,kad->agqd/dot_general | solution.py:163
  168.4 1.8 fusion.47
  170.2 2.8 bitcast_add_fusion.5
  174.0 3.1 gather_fusion
  177.4 5.6 %fusion.46 = (f32[4,8,128]{2,1,0:T(8,128)S(1)}, f32[4,512,128,8]{2,1,3,0:T(8,128)}) fusion(pred[128,512]{0,1:T(8,128)(4,1)S(1)} %compare_and_fusion.3, bf16[512,4,64,1]{0,2,3,1:T(8,128)(2,1)S(1)} %bitcast.126, bf16[128,4,8,64]{0,3,2,1:T(8,128)(2,1)} %get-tuple-element.422), kind=kOutput, calls=%fused_computation.8.clone.1 | convolution fusion | flops 274722816 | bytes 9256960 | tf_op jit(solution)/shard_map/while/body/eval_jaxpr/qagd,kad->agqk/dot_general | solution.py:150
  184.8 6.6 %fusion.48 = f32[4,8,128,64]{2,3,1,0:T(8,128)} fusion(bf16[512,4,64,1]{0,2,3,1:T(8,128)(2,1)} %bitcast.129, f32[4,512,128,8]{2,1,3,0:T(8,128)} %get-tuple-element.384, f32[4,8,128]{2,1,0:T(8,128)S(1)} %bitcast.127, pred[128,512]{0,1:T(8,128)(4,1)S(1)} %compare_and_fusion.3), kind=kOutput, calls=%fused_computation.9.clone.1 | convolution fusion | flops 276824064 | bytes 9781248 | tf_op jit(solution)/shard_map/while/body/eval_jaxpr/agqk,kad->agqd/dot_general | solution.py:163
  191.4 1.8 fusion.47
  193.2 2.8 bitcast_add_fusion.5
  196.0 1.0 constant_dynamic-slice_fusion.5
  197.0 3.1 gather_fusion
  200.4 5.6 %fusion.46 = (f32[4,8,128]{2,1,0:T(8,128)S(1)}, f32[4,512,128,8]{2,1,3,0:T(8,128)}) fusion(pred[128,512]{0,1:T(8,128)(4,1)S(1)} %compare_and_fusion.3, bf16[512,4,64,1]{0,2,3,1:T(8,128)(2,1)S(1)} %bitcast.126, bf16[128,4,8,64]{0,3,2,1:T(8,128)(2,1)} %get-tuple-element.422), kind=kOutput, calls=%fused_computation.8.clone.1 | convolution fusion | flops 274722816 | bytes 9256960 | tf_op jit(solution)/shard_map/while/body/eval_jaxpr/qagd,kad->agqk/dot_general | solution.py:150
  207.8 6.6 %fusion.48 = f32[4,8,128,64]{2,3,1,0:T(8,128)} fusion(bf16[512,4,64,1]{0,2,3,1:T(8,128)(2,1)} %bitcast.129, f32[4,512,128,8]{2,1,3,0:T(8,128)} %get-tuple-element.384, f32[4,8,128]{2,1,0:T(8,128)S(1)} %bitcast.127, pred[128,512]{0,1:T(8,128)(4,1)S(1)} %compare_and_fusion.3), kind=kOutput, calls=%fused_computation.9.clone.1 | convolution fusion | flops 276824064 | bytes 9781248 | tf_op jit(solution)/shard_map/while/body/eval_jaxpr/agqk,kad->agqd/dot_general | solution.py:163
  214.4 1.8 fusion.47
  216.2 2.8 bitcast_add_fusion.5
  220.0 3.1 gather_fusion
  223.4 5.6 %fusion.46 = (f32[4,8,128]{2,1,0:T(8,128)S(1)}, f32[4,512,128,8]{2,1,3,0:T(8,128)}) fusion(pred[128,512]{0,1:T(8,128)(4,1)S(1)} %compare_and_fusion.3, bf16[512,4,64,1]{0,2,3,1:T(8,128)(2,1)S(1)} %bitcast.126, bf16[128,4,8,64]{0,3,2,1:T(8,128)(2,1)} %get-tuple-element.422), kind=kOutput, calls=%fused_computation.8.clone.1 | convolution fusion | flops 274722816 | bytes 9256960 | tf_op jit(solution)/shard_map/while/body/eval_jaxpr/qagd,kad->agqk/dot_general | solution.py:150
  230.8 6.6 %fusion.48 = f32[4,8,128,64]{2,3,1,0:T(8,128)} fusion(bf16[512,4,64,1]{0,2,3,1:T(8,128)(2,1)} %bitcast.129, f32[4,512,128,8]{2,1,3,0:T(8,128)} %get-tuple-element.384, f32[4,8,128]{2,1,0:T(8,128)S(1)} %bitcast.127, pred[128,512]{0,1:T(8,128)(4,1)S(1)} %compare_and_fusion.3), kind=kOutput, calls=%fused_computation.9.clone.1 | convolution fusion | flops 276824064 | bytes 9781248 | tf_op jit(solution)/shard_map/while/body/eval_jaxpr/agqk,kad->agqd/dot_general | solution.py:163
  237.3 1.8 fusion.47
  239.2 2.8 bitcast_add_fusion.5
  243.0 3.1 gather_fusion
  246.4 5.6 %fusion.46 = (f32[4,8,128]{2,1,0:T(8,128)S(1)}, f32[4,512,128,8]{2,1,3,0:T(8,128)}) fusion(pred[128,512]{0,1:T(8,128)(4,1)S(1)} %compare_and_fusion.3, bf16[512,4,64,1]{0,2,3,1:T(8,128)(2,1)S(1)} %bitcast.126, bf16[128,4,8,64]{0,3,2,1:T(8,128)(2,1)} %get-tuple-element.422), kind=kOutput, calls=%fused_computation.8.clone.1 | convolution fusion | flops 274722816 | bytes 9256960 | tf_op jit(solution)/shard_map/while/body/eval_jaxpr/qagd,kad->agqk/dot_general | solution.py:150
  253.8 6.6 %fusion.48 = f32[4,8,128,64]{2,3,1,0:T(8,128)} fusion(bf16[512,4,64,1]{0,2,3,1:T(8,128)(2,1)} %bitcast.129, f32[4,512,128,8]{2,1,3,0:T(8,128)} %get-tuple-element.384, f32[4,8,128]{2,1,0:T(8,128)S(1)} %bitcast.127, pred[128,512]{0,1:T(8,128)(4,1)S(1)} %compare_and_fusion.3), kind=kOutput, calls=%fused_computation.9.clone.1 | convolution fusion | flops 276824064 | bytes 9781248 | tf_op jit(solution)/shard_map/while/body/eval_jaxpr/agqk,kad->agqd/dot_general | solution.py:163
  260.3 1.8 fusion.47
  262.2 2.8 bitcast_add_fusion.5
  266.0 3.1 gather_fusion
  269.4 5.6 %fusion.46 = (f32[4,8,128]{2,1,0:T(8,128)S(1)}, f32[4,512,128,8]{2,1,3,0:T(8,128)}) fusion(pred[128,512]{0,1:T(8,128)(4,1)S(1)} %compare_and_fusion.3, bf16[512,4,64,1]{0,2,3,1:T(8,128)(2,1)S(1)} %bitcast.126, bf16[128,4,8,64]{0,3,2,1:T(8,128)(2,1)} %get-tuple-element.422), kind=kOutput, calls=%fused_computation.8.clone.1 | convolution fusion | flops 274722816 | bytes 9256960 | tf_op jit(solution)/shard_map/while/body/eval_jaxpr/qagd,kad->agqk/dot_general | solution.py:150
  276.8 6.6 %fusion.48 = f32[4,8,128,64]{2,3,1,0:T(8,128)} fusion(bf16[512,4,64,1]{0,2,3,1:T(8,128)(2,1)} %bitcast.129, f32[4,512,128,8]{2,1,3,0:T(8,128)} %get-tuple-element.384, f32[4,8,128]{2,1,0:T(8,128)S(1)} %bitcast.127, pred[128,512]{0,1:T(8,128)(4,1)S(1)} %compare_and_fusion.3), kind=kOutput, calls=%fused_computation.9.clone.1 | convolution fusion | flops 276824064 | bytes 9781248 | tf_op jit(solution)/shard_map/while/body/eval_jaxpr/agqk,kad->agqd/dot_general | solution.py:163
  283.3 1.8 fusion.47
  285.2 2.8 bitcast_add_fusion.5
  289.0 3.1 gather_fusion
  292.4 5.6 %fusion.46 = (f32[4,8,128]{2,1,0:T(8,128)S(1)}, f32[4,512,128,8]{2,1,3,0:T(8,128)}) fusion(pred[128,512]{0,1:T(8,128)(4,1)S(1)} %compare_and_fusion.3, bf16[512,4,64,1]{0,2,3,1:T(8,128)(2,1)S(1)} %bitcast.126, bf16[128,4,8,64]{0,3,2,1:T(8,128)(2,1)} %get-tuple-element.422), kind=kOutput, calls=%fused_computation.8.clone.1 | convolution fusion | flops 274722816 | bytes 9256960 | tf_op jit(solution)/shard_map/while/body/eval_jaxpr/qagd,kad->agqk/dot_general | solution.py:150
  299.8 6.6 %fusion.48 = f32[4,8,128,64]{2,3,1,0:T(8,128)} fusion(bf16[512,4,64,1]{0,2,3,1:T(8,128)(2,1)} %bitcast.129, f32[4,512,128,8]{2,1,3,0:T(8,128)} %get-tuple-element.384, f32[4,8,128]{2,1,0:T(8,128)S(1)} %bitcast.127, pred[128,512]{0,1:T(8,128)(4,1)S(1)} %compare_and_fusion.3), kind=kOutput, calls=%fused_computation.9.clone.1 | convolution fusion | flops 276824064 | bytes 9781248 | tf_op jit(solution)/shard_map/while/body/eval_jaxpr/agqk,kad->agqd/dot_general | solution.py:163
  306.3 1.8 fusion.47
  308.1 2.8 bitcast_add_fusion.5
  312.5 4.7 %all-to-all-start = ((f32[16,1,256]{2,1,0:T(1,128)}), f32[16,1,256]{2,1,0:T(1,128)S(1)}, u32[]{:S(2)}, u32[]{:S(2)}) async-start(f32[16,1,256]{2,1,0:T(1,128)} %reshape.354), calls=%async_computation | async-start | bytes 32768 | tf_op jit(solution)/shard_map/all_to_all | solution.py:41
  317.2 1.4 divide_convert_fusion
  318.6 1.0 copy.73
  319.6 4.1 %all-to-all-done = f32[16,1,256]{2,1,0:T(1,128)S(1)} async-done(((f32[16,1,256]{2,1,0:T(1,128)}), f32[16,1,256]{2,1,0:T(1,128)S(1)}, u32[]{:S(2)}, u32[]{:S(2)}) %all-to-all-start) | async-done | bytes 16416 | tf_op jit(solution)/shard_map/all_to_all | solution.py:41
  325.1 5.1 %all_to_all.10 = f32[2,1,2048]{2,1,0:T(1,128)S(1)} all-to-all(f32[2,1,2048]{2,1,0:T(1,128)S(1)} %reshape.356), channel_id=1, replica_groups=mesh['dp'=4,'cp_0'=4,'cp_1'=4,'cp_2'=2] {'cp_2'}, dimensions={0} | all-to-all | bytes 32768 | tf_op jit(solution)/shard_map/all_to_all | solution.py:41
  (157 shorter events, 28.4 us)
Async XLA Ops:
  7.2 26.9 %copy-start = (bf16[2880,512]{1,0:T(8,128)(2,1)S(1)}, bf16[2880,512]{1,0:T(8,128)(2,1)}, u32[]{:S(2)}) copy-start(bf16[2880,512]{1,0:T(8,128)(2,1)} %param.13) | copy-start | bytes 8847364
  7.2 113.6 %all-gather.3.cloned.1.call-start = ((), (), s32[]{:S(2)}) async-start(), calls=%async_computation.2 | async-start | bytes 2162688 | tf_op jit(solution)/shard_map/all_gather | solution.py:177
  37.5 89.8 %all-gather.5.cloned.1.call-start = ((), (), s32[]{:S(2)}) async-start(), calls=%async_computation.3 | async-start | bytes 2162688 | tf_op jit(solution)/shard_map/all_gather | solution.py:178
  73.3 18.2 %copy-start.3 = (s32[1,1,32]{2,1,0:T(1,128)S(1)}, s32[1,1,32]{2,1,0:T(1,128)}, u32[]{:S(2)}) copy-start(s32[1,1,32]{2,1,0:T(1,128)} %param.16) | copy-start | bytes 388
  73.3 38.7 %copy-start.2 = (f32[2880]{0:T(1024)S(1)}, f32[2880]{0:T(1024)}, u32[]{:S(2)}) copy-start(f32[2880]{0:T(1024)} %param.11) | copy-start | bytes 34564
  112.0 8.3 %copy-start.5 = (s32[1,128]{1,0:T(1,128)S(1)}, s32[1,128]{1,0:T(1,128)}, u32[]{:S(2)}) copy-start(s32[1,128]{1,0:T(1,128)} %param.17) | copy-start | bytes 1540
  112.0 15.3 %copy-start.4 = (f32[32]{0:T(128)S(1)}, f32[32]{0:T(128)}, u32[]{:S(2)}) copy-start(f32[32]{0:T(128)} %param.14) | copy-start | bytes 388
  139.1 6.6 %copy-start.1 = (f32[4,512,128,8]{2,1,3,0:T(8,128)S(1)}, f32[4,512,128,8]{2,1,3,0:T(8,128)}, u32[]{:S(2)}) copy-start(f32[4,512,128,8]{2,1,3,0:T(8,128)} %get-tuple-element.384) | copy-start | bytes 25165828 | tf_op jit(solution)/shard_map/while
  161.8 6.6 %copy-start.1 = (f32[4,512,128,8]{2,1,3,0:T(8,128)S(1)}, f32[4,512,128,8]{2,1,3,0:T(8,128)}, u32[]{:S(2)}) copy-start(f32[4,512,128,8]{2,1,3,0:T(8,128)} %get-tuple-element.384) | copy-start | bytes 25165828 | tf_op jit(solution)/shard_map/while
  184.8 6.6 %copy-start.1 = (f32[4,512,128,8]{2,1,3,0:T(8,128)S(1)}, f32[4,512,128,8]{2,1,3,0:T(8,128)}, u32[]{:S(2)}) copy-start(f32[4,512,128,8]{2,1,3,0:T(8,128)} %get-tuple-element.384) | copy-start | bytes 25165828 | tf_op jit(solution)/shard_map/while
  207.8 6.6 %copy-start.1 = (f32[4,512,128,8]{2,1,3,0:T(8,128)S(1)}, f32[4,512,128,8]{2,1,3,0:T(8,128)}, u32[]{:S(2)}) copy-start(f32[4,512,128,8]{2,1,3,0:T(8,128)} %get-tuple-element.384) | copy-start | bytes 25165828 | tf_op jit(solution)/shard_map/while
  230.8 6.6 %copy-start.1 = (f32[4,512,128,8]{2,1,3,0:T(8,128)S(1)}, f32[4,512,128,8]{2,1,3,0:T(8,128)}, u32[]{:S(2)}) copy-start(f32[4,512,128,8]{2,1,3,0:T(8,128)} %get-tuple-element.384) | copy-start | bytes 25165828 | tf_op jit(solution)/shard_map/while
  253.8 6.6 %copy-start.1 = (f32[4,512,128,8]{2,1,3,0:T(8,128)S(1)}, f32[4,512,128,8]{2,1,3,0:T(8,128)}, u32[]{:S(2)}) copy-start(f32[4,512,128,8]{2,1,3,0:T(8,128)} %get-tuple-element.384) | copy-start | bytes 25165828 | tf_op jit(solution)/shard_map/while
  276.8 6.6 %copy-start.1 = (f32[4,512,128,8]{2,1,3,0:T(8,128)S(1)}, f32[4,512,128,8]{2,1,3,0:T(8,128)}, u32[]{:S(2)}) copy-start(f32[4,512,128,8]{2,1,3,0:T(8,128)} %get-tuple-element.384) | copy-start | bytes 25165828 | tf_op jit(solution)/shard_map/while
  299.8 6.6 %copy-start.1 = (f32[4,512,128,8]{2,1,3,0:T(8,128)S(1)}, f32[4,512,128,8]{2,1,3,0:T(8,128)}, u32[]{:S(2)}) copy-start(f32[4,512,128,8]{2,1,3,0:T(8,128)} %get-tuple-element.384) | copy-start | bytes 25165828 | tf_op jit(solution)/shard_map/while
  312.5 11.1 %all-to-all-start = ((f32[16,1,256]{2,1,0:T(1,128)}), f32[16,1,256]{2,1,0:T(1,128)S(1)}, u32[]{:S(2)}, u32[]{:S(2)}) async-start(f32[16,1,256]{2,1,0:T(1,128)} %reshape.354), calls=%async_computation | async-start | bytes 32768 | tf_op jit(solution)/shard_map/all_to_all | solution.py:41
Sparse Core Ops, SparseCore 0:
  37.6 44.3 all-gather.2
  84.2 43.0 all-gather.4
where the time goes:
time: 341 us; the launch traced here: 339 us
  matrix products  107 us (31%)
  blocking collectives  83.6 us (25%)
  local copies, waits for them, and re-layouts  70 us (21%)
  other arithmetic  47.6 us (14%)
  between operations  15 us (4%)
  waiting for transfers between devices  10.6 us (3%)
  starting transfers between devices  4.76 us (1%)
    dot_general x8, matrix products, attend_block(): jnp.einsum('agqk,kad->agqd', weights, value_part.reshape(key_count, kv_he...  52.5 us
    dot_general x8, matrix products, attend_block(): jnp.einsum('qagd,kad->agqk', query_heads, key_part.reshape(key_count, kv_...  44.5 us
    psum x4, blocking collectives, by_axis(): x = lax.psum(x, axis)  33.9 us
    gather x8, local copies, waits for them, and re-layouts, attend_block(): key_doc = doc_index[places]  25.1 us
    all_gather x1, blocking collectives, body(): lax.all_gather(document_ids, CP, axis=1, tiled=True)  24.4 us
    add x8, other arithmetic, attend_block(): return (new_top, new_total, row_sums * shrink[..., None] + mixed_values)  22.3 us
    all_gather x1, blocking collectives, body(): lax.all_gather(block_owner, CP, axis=1, tiled=True)  20.2 us
    unnamed x18, local copies, waits for them, and re-layouts  19.1 us
  transfers between devices with their start and end apart: 3, of which 2 were waited for; matrix products, arithmetic and copies ran while one was open for 9% of the time, Pallas kernels for 0%

commit v1 on v0

v1 whole, which is shorter than its diff:
```python
import functools
import math

import jax
import jax.numpy as jnp
import numpy as np
from jax import lax
from jax.experimental import pallas as pl
from jax.experimental.pallas import tpu as pltpu
from jax.sharding import PartitionSpec as P

MESH = pl.DeviceIdType.MESH
HEAD_DIM = 64
DOC_MOST = 1024
ROPE_BASE = 150000.0
NORM_EPS = 1e-05
MASKED = -1e30
LOG2E = 1.4426950408889634
LN2 = 0.6931471805599453
F32 = jnp.float32
BF16 = jnp.bfloat16
NT = (((1,), (1,)), ((), ()))
Q_CHUNK = 256


def iota(shape, dim):
    return lax.broadcasted_iota(jnp.int32, shape, dim)


def exact_dot(a, b, dims=(((1,), (0,)), ((), ()))):
    return lax.dot_general(a, b, dims, precision=lax.Precision.HIGHEST, preferred_element_type=F32)


def cos_sin(angle):
    k = jnp.floor(angle * (2.0 / math.pi) + 0.5)
    r = ((angle - k * 1.5703125) - k * 4.837512969970703125e-4) - k * 7.549789954891882e-8
    z = r * r
    s = ((-1.9515295891e-4 * z + 8.3321608736e-3) * z - 1.6666654611e-1) * z * r + r
    c = ((2.443315711809948e-5 * z - 1.388731625493765e-3) * z + 4.166664568298827e-2) * z * z - 0.5 * z + 1.0
    q = k.astype(jnp.int32) & 3
    odd = (q & 1) == 1
    cosine = jnp.where(odd, s, c)
    sine = jnp.where(odd, c, s)
    cosine = jnp.where((q == 1) | (q == 2), -cosine, cosine)
    sine = jnp.where(q >= 2, -sine, sine)
    return cosine, sine


def swap_halves(x, low):
    return jnp.where(low, pltpu.roll(x, 96, 1), pltpu.roll(x, 32, 1))


def kernel(
    shape,
    groups,
    hidden_hbm, gain_hbm, qw_hbm, kvw_hbm, sink_ref, docs_ref, owner_ref, mask_ref, freq_ref,
    att_ref, lse_out_ref, tw_ref,
    hid, gain, kvw, qw, normed, qraw, qz, kbuf, vbuf, bias,
    docs_buf, cnt_send, cnt_buf, m_ref, acc_ref, lse_ref, comb_send, comb,
    load_sem, qw_sem,
    doc_ssem, doc_rsem, kv_ssem, kv_rsem, cnt_ssem, cnt_rsem, lse_ssem, lse_rsem,
):
    rows, width, heads, kv_heads, shards, dps = shape
    back = DOC_MOST // rows
    per_kv = heads // kv_heads
    block_rows = rows // shards
    me = lax.axis_index("cp")
    my_dp = lax.axis_index("dp")
    qdim = heads * HEAD_DIM
    n_chunks = qdim // Q_CHUNK
    pairs = heads // 2

    def ahead(k):
        return lax.rem(me + k, shards)

    loads = [
        pltpu.make_async_copy(hidden_hbm, hid, load_sem.at[0]),
        pltpu.make_async_copy(gain_hbm, gain, load_sem.at[1]),
        pltpu.make_async_copy(kvw_hbm, kvw, load_sem.at[2]),
    ]
    for c in loads:
        c.start()
    q_loads = [
        pltpu.make_async_copy(qw_hbm.at[:, pl.ds(i * Q_CHUNK, Q_CHUNK)], qw.at[i], qw_sem.at[i])
        for i in range(n_chunks)
    ]
    for c in q_loads:
        c.start()

    barrier = pltpu.get_barrier_semaphore()

    def greet(k, carry):
        pl.semaphore_signal(barrier, inc=1, device_id={"cp": ahead(k)}, device_id_type=MESH)
        return carry

    lax.fori_loop(1, shards, greet, 0)
    for k in range(1, dps):
        pl.semaphore_signal(
            barrier, inc=1, device_id={"dp": lax.rem(my_dp + k, dps)}, device_id_type=MESH
        )

    own_docs = docs_ref[...]
    docs_buf[back] = own_docs
    flags = mask_ref[...].astype(F32)
    cnt_row = jnp.broadcast_to(jnp.sum(flags, axis=1, keepdims=True), (1, rows))
    cnt_send[0] = cnt_row
    cnt_buf[0] = cnt_row

    loads[0].wait()
    loads[1].wait()
    x = hid[...].astype(F32)
    inv = lax.rsqrt(jnp.sum(x * x, axis=1, keepdims=True) * (1.0 / width) + NORM_EPS)
    normed[...] = (x * inv * gain[...]).astype(BF16)

    loads[2].wait()
    kv = jnp.dot(normed[...], kvw[...], preferred_element_type=F32)
    kv_width = kv_heads * HEAD_DIM
    for t in range(kv_heads // 2):
        v_t = kv[:, kv_width + t * 128:kv_width + (t + 1) * 128].T.astype(BF16)
        vbuf[back, 2 * t] = v_t[:HEAD_DIM]
        vbuf[back, 2 * t + 1] = v_t[HEAD_DIM:]

    pl.semaphore_wait(barrier, shards - 1 + dps - 1)

    sends = []

    def send(src, dst, ssem, rsem, device):
        c = pltpu.make_async_remote_copy(
            src_ref=src, dst_ref=dst, send_sem=ssem, recv_sem=rsem,
            device_id=device, device_id_type=MESH,
        )
        c.start()
        sends.append(c)
        return c

    doc_copies = {}
    for k in range(1, back + 1):
        doc_copies[k] = send(
            docs_buf.at[back], docs_buf.at[back - k], doc_ssem.at[k - 1], doc_rsem.at[k - 1],
            {"cp": ahead(k)},
        )
    cnt_copies = []
    for k in range(1, dps):
        cnt_copies.append(send(
            cnt_send.at[0], cnt_buf.at[k], cnt_ssem.at[k - 1], cnt_rsem.at[k - 1],
            {"dp": lax.rem(my_dp + k, dps)},
        ))
    v_copies, k_copies = {}, {}
    for k in range(1, back + 1):
        v_copies[k] = send(
            vbuf.at[back], vbuf.at[back - k], kv_ssem.at[0, k - 1], kv_rsem.at[0, k - 1], {"cp": ahead(k)}
        )

    for i in range(n_chunks):
        q_loads[i].wait()
        qraw[:, i * Q_CHUNK:(i + 1) * Q_CHUNK] = jnp.dot(normed[...], qw[i], preferred_element_type=F32)

    for k in range(1, back + 1):
        doc_copies[k].wait_recv()
    square = (rows, 128)
    lane = iota(square, 1)
    sub = iota(square, 0)
    own_row = jnp.broadcast_to(own_docs.astype(F32), square)
    own_col = own_row.T
    count = jnp.zeros(square, F32)
    for b in range(back + 1):
        window_docs = docs_buf[b].astype(F32)
        if b < back:
            window_docs = jnp.where(me >= back - b, window_docs, -1.0)
        count = count + (jnp.broadcast_to(window_docs, square) < own_col).astype(F32)
    start_col = jnp.broadcast_to(jnp.sum(count, axis=1, keepdims=True), square)
    within = (sub + back * rows).astype(F32) - start_col
    cosine, sine = cos_sin(within * freq_ref[...])
    low = (lane % HEAD_DIM) < HEAD_DIM // 2
    sine = jnp.where(low, -sine, sine)

    for t in range(kv_heads // 2):
        u = kv[:, t * 128:(t + 1) * 128]
        kbuf[back, t] = (u * cosine + swap_halves(u, low) * sine).astype(BF16)
    for k in range(1, back + 1):
        k_copies[k] = send(
            kbuf.at[back], kbuf.at[back - k], kv_ssem.at[1, k - 1], kv_rsem.at[1, k - 1], {"cp": ahead(k)}
        )

    scale = HEAD_DIM ** (-0.5)
    q_cos, q_sin = cosine * scale, sine * scale
    left = lane < HEAD_DIM
    for j in range(pairs):
        u = qraw[:, j * 128:(j + 1) * 128]
        y = u * q_cos + swap_halves(u, low) * q_sin
        a = (2 * j) // per_kv
        if a % 2 == 0:
            even = jnp.where(left, y, 0.0)
            odd = jnp.where(left, pltpu.roll(y, 64, 1), 0.0)
        else:
            even = jnp.where(left, 0.0, pltpu.roll(y, 64, 1))
            odd = jnp.where(left, 0.0, y)
        qz[j, :rows] = even.astype(BF16)
        qz[j, rows:] = odd.astype(BF16)

    start_row = start_col.T
    for b in range(back + 1):
        place = (sub + b * rows).astype(F32)
        allowed = place >= start_row
        if b == back:
            allowed = allowed & (sub <= lane)
        bias[b] = jnp.where(allowed, 0.0, MASKED)

    ones_rows = jnp.ones((16, 128), BF16)
    pair_lane = iota((1, 2 * rows), 1) < rows
    acc_rows = HEAD_DIM + 16
    for gi, group in enumerate(groups):
        for b in group:
            if b < back:
                v_copies[back - b].wait_recv()
                k_copies[back - b].wait_recv()
        first, last = gi == 0, gi == len(groups) - 1

        def one_pair(j, carry, group=group, first=first, last=last):
            a = j // (per_kv // 2)
            q2 = qz[j]
            scores = []
            top = None
            for b in group:
                s = lax.dot_general(kbuf[b, a // 2], q2, NT, preferred_element_type=F32)
                bb = bias[b]
                s = s * LOG2E + jnp.concatenate([bb, bb], axis=1)
                scores.append(s)
                part = jnp.max(s.reshape(rows // 8, 8, 2 * rows), axis=0)
                top = part if top is None else jnp.maximum(top, part)
            top = jnp.max(top, axis=0, keepdims=True)
            if first:
                old = jnp.where(pair_lane, sink_ref[2 * j], sink_ref[2 * j + 1]) * LOG2E
            else:
                old = m_ref[j][:1]
            new = jnp.maximum(old, top)
            weights = [jnp.exp2(s - new).astype(BF16) for s in scores]
            vt = jnp.concatenate([jnp.concatenate([vbuf[b, a], ones_rows], axis=0) for b in group], axis=1)
            mixed = jnp.dot(vt, jnp.concatenate(weights, axis=0), preferred_element_type=F32)
            shrink = jnp.exp2(old - new)
            if first:
                acc = mixed + jnp.where(iota((acc_rows, 2 * rows), 0) >= HEAD_DIM, shrink, 0.0)
            else:
                acc = acc_ref[j] * shrink + mixed
            if last:
                total = acc[HEAD_DIM:HEAD_DIM + 1]
                out = acc[:HEAD_DIM] * (1.0 / total)
                out = jnp.concatenate([out[:, :rows], out[:, rows:]], axis=0).T
                att_ref[:, pl.ds(pl.multiple_of(j * 128, 128), 128)] = out.astype(BF16)
                lse = (new + jnp.log2(total)) * LN2
                lse_ref[pl.ds(2 * j, 1), :] = lse[:, :rows]
                lse_ref[pl.ds(2 * j + 1, 1), :] = lse[:, rows:]
            else:
                acc_ref[j] = acc
                m_ref[j] = jnp.broadcast_to(new, (8, 2 * rows))
            return carry

        lax.fori_loop(0, pairs, one_pair, 0)

    for c in cnt_copies:
        c.wait_recv()
    cnt = cnt_buf[0]
    for k in range(1, dps):
        cnt = cnt + cnt_buf[k]

    spread = (iota((shards, rows), 1) // block_rows == iota((shards, rows), 0)).astype(F32)
    owner_row = jnp.broadcast_to(owner_ref[...].astype(F32), (8, shards))
    owner_wide = exact_dot(owner_row, spread)[:1]
    chosen = (jnp.broadcast_to(owner_wide, (shards, rows)) == iota((shards, rows), 0).astype(F32)).astype(F32)
    wide = block_rows * heads
    lse4 = jnp.concatenate([lse_ref[...]] * block_rows, axis=0)
    lse4 = jnp.where(iota((wide, rows), 1) % block_rows == iota((wide, rows), 0) // heads, lse4, 0.0)
    rows_out = exact_dot(chosen, lse4, NT)
    comb_send[:, 0, :] = rows_out
    comb_send[:, 1, :] = jnp.broadcast_to(cnt, (shards, rows))
    comb[me] = comb_send[me]

    def lse_copy(k):
        return pltpu.make_async_remote_copy(
            src_ref=comb_send.at[ahead(k)], dst_ref=comb.at[me],
            send_sem=lse_ssem.at[k], recv_sem=lse_rsem.at[k],
            device_id={"cp": ahead(k)}, device_id_type=MESH,
        )

    def lse_send(k, carry):
        lse_copy(k).start()
        return carry

    def lse_wait(k, carry):
        lse_copy(k).wait_recv()
        return carry

    def lse_done(k, carry):
        lse_copy(k).wait_send()
        return carry

    lax.fori_loop(1, shards, lse_send, 0)
    lax.fori_loop(1, shards, lse_wait, 0)

    got = comb[:, 0, :]
    totals = jnp.sum(comb[:, 1, :], axis=0, keepdims=True)
    back_spread = (iota((rows, shards), 0) // block_rows == iota((rows, shards), 1)).astype(F32)
    wide_got = exact_dot(back_spread, got)
    wide_got = jnp.where(iota((rows, wide), 0) % block_rows == iota((rows, wide), 1) // heads, wide_got, 0.0)
    pick = (iota((heads, wide), 1) % heads == iota((heads, wide), 0)).astype(F32)
    lse_out_ref[...] = exact_dot(pick, wide_got, NT)
    tw_ref[...] = flags * (float(dps * shards * rows) / totals)

    for c in sends:
        c.wait_send()
    lax.fori_loop(1, shards, lse_done, 0)


def solution(mesh):
    dps, shards = mesh.shape["dp"], mesh.shape["cp"]
    half = HEAD_DIM // 2
    freq_np = ROPE_BASE ** (-(np.arange(128) % half).astype(np.float64) / half)

    def body(hidden, norm_gain, query_weight, keyval_weight, sink_logits, document_ids, block_owner, loss_mask):
        rows, width = hidden.shape[1:]
        heads = sink_logits.shape[0]
        kv_heads = keyval_weight.shape[1] // (2 * HEAD_DIM)
        qdim = heads * HEAD_DIM
        back = DOC_MOST // rows
        slots = back + 1
        pairs = heads // 2
        groups = ((back,), tuple(range(back - 1, back // 2 - 1, -1)), tuple(range(back // 2 - 1, -1, -1)))
        shape = (rows, width, heads, kv_heads, shards, dps)
        any_spec = pl.BlockSpec(memory_space=pl.ANY)
        vm = pl.BlockSpec(memory_space=pltpu.VMEM)
        dma = pltpu.SemaphoreType.DMA
        att, lse, tw = pl.pallas_call(
            functools.partial(kernel, shape, groups),
            name="attention_step",
            out_shape=(
                jax.ShapeDtypeStruct((rows, qdim), BF16),
                jax.ShapeDtypeStruct((heads, rows), F32),
                jax.ShapeDtypeStruct((1, rows), F32),
            ),
            in_specs=[any_spec] * 4 + [pl.BlockSpec(memory_space=pltpu.SMEM)] + [vm] * 4,
            out_specs=(vm, vm, vm),
            scratch_shapes=[
                pltpu.VMEM((rows, width), BF16),
                pltpu.VMEM((1, width), F32),
                pltpu.VMEM((width, keyval_weight.shape[1]), BF16),
                pltpu.VMEM((qdim // Q_CHUNK, width, Q_CHUNK), BF16),
                pltpu.VMEM((rows, width), BF16),
                pltpu.VMEM((rows, qdim), F32),
                pltpu.VMEM((pairs, 2 * rows, 128), BF16),
                pltpu.VMEM((slots, kv_heads // 2, rows, 128), BF16),
                pltpu.VMEM((slots, kv_heads, HEAD_DIM, rows), BF16),
                pltpu.VMEM((slots, rows, rows), F32),
                pltpu.VMEM((slots, 1, rows), jnp.int32),
                pltpu.VMEM((1, 1, rows), F32),
                pltpu.VMEM((dps, 1, rows), F32),
                pltpu.VMEM((pairs, 8, 2 * rows), F32),
                pltpu.VMEM((pairs, HEAD_DIM + 16, 2 * rows), F32),
                pltpu.VMEM((heads, rows), F32),
                pltpu.VMEM((shards, 2, rows), F32),
                pltpu.VMEM((shards, 2, rows), F32),
                dma((3,)), dma((qdim // Q_CHUNK,)),
                dma((back,)), dma((back,)),
                dma((2, back)), dma((2, back)),
                dma((dps,)), dma((dps,)),
                dma((shards,)), dma((shards,)),
            ],
            compiler_params=pltpu.CompilerParams(
                collective_id=0, has_side_effects=True, vmem_limit_bytes=56 * 1024 * 1024
            ),
        )(
            hidden[0], norm_gain.reshape(1, width), query_weight, keyval_weight, sink_logits,
            document_ids, block_owner[0], loss_mask,
            jnp.asarray(freq_np.reshape(1, 128), F32),
        )
        return att[None], lse[None], tw

    return jax.shard_map(
        body,
        mesh=mesh,
        in_specs=(
            P("dp", "cp", None), P(), P(), P(), P(), P("dp", "cp"), P("dp", "cp", None), P("dp", "cp"),
        ),
        out_specs=(P("dp", "cp", None), P("dp", None, "cp"), P("dp", "cp")),
        check_vma=False,
    )
```

time: 341 us -> 63.3 us (0.19)
  matrix products: 107 us -> 0 us
  blocking collectives: 83.6 us -> 0 us
  local copies, waits for them, and re-layouts: 70 us -> 7.92 us
  Pallas kernels: 0 us -> 54.4 us
  other arithmetic: 47.6 us -> 0 us
  between operations: 15 us -> 0.64 us
  waiting for transfers between devices: 10.6 us -> 0 us
  starting transfers between devices: 4.76 us -> 0 us
    dot_general x18 -> x0, matrix products: 107 us -> none  [the longest x8 52.5 us: attend_block(): jnp.einsum('agqk,kad->agqd', weights, value_part.reshape(key_count, kv_he...]
    pallas_call x0 -> x1, Pallas kernels: none -> 54.4 us  [body(): pl.pallas_call(functools.partial(kernel, shape, groups), name='attention_...]
    all_gather x2 -> x0, blocking collectives: 44.6 us -> none  [the longest x1 24.4 us: body(): lax.all_gather(document_ids, CP, axis=1, tiled=True)]
    psum x4 -> x0, blocking collectives: 33.9 us -> none  [by_axis(): x = lax.psum(x, axis)]
    gather x10 -> x0, local copies, waits for them, and re-layouts: 26.9 us -> none  [the longest x8 25.1 us: attend_block(): key_doc = doc_index[places]]
    add x33 -> x0, other arithmetic: 22.5 us -> none  [the longest x8 22.3 us: attend_block(): return (new_top, new_total, row_sums * shrink[..., None] + mixed_values)]
    dynamic_slice x24 -> x0, local copies, waits for them, and re-layouts: 22.2 us -> none  [the longest x16 14.5 us: one_step(): value_part = lax.dynamic_slice_in_dim(value_piece, offset, sub_rows, 0)]
    reduce_sum x11 -> x0, other arithmetic: 17.4 us -> none  [the longest x8 14.4 us: attend_block(): new_total = row_total * shrink + jnp.sum(exp_scores, axis=-1)]
  transfers between devices with their start and end apart: 3 -> 0, of which waited for: 2 -> 0; matrix products, arithmetic and copies ran while one was open for 9% -> 0% of each run, Pallas kernels for 0% -> 0%
where the time goes in v1:
time: 63.3 us; the launch traced here: 62.9 us
  Pallas kernels  54.4 us (86%)
  local copies, waits for them, and re-layouts  7.92 us (13%)
  between operations  0.64 us (1%)
    pallas_call x1, Pallas kernels, body(): pl.pallas_call(functools.partial(kernel, shape, groups), name='attention_...  54.4 us
    unnamed x4, local copies, waits for them, and re-layouts  6.6 us
    reshape x1, local copies, waits for them, and re-layouts, body(): norm_gain.reshape(1, width)  1.32 us

profile of v1, /device:TPU:1, one launch (start us, length us, event | category | flops | bytes accessed | tf_op | source)
XLA Modules:
  0.0 62.9 jit_solution(5228913287405680450)
XLA Ops:
  0.6 1.3 %reshape.9.gain_hbm = f32[1,2880]{1,0:T(1,128)} reshape(f32[2880]{0:T(1024)} %param.10) | data formatting | bytes 23040 | tf_op jit(solution)/shard_map/reshape | solution.py:371
  1.9 2.3 %copy.12 = bf16[1,128,2880]{2,1,0:T(8,128)(2,1)} copy(bf16[1,128,2880]{1,2,0:T(8,128)(2,1)} %param.9) | data formatting | bytes 1474560 | tf_op args[0]
  4.2 54.4 %attention_step.1 = (bf16[128,2048]{1,0:T(8,128)(2,1)}, f32[32,128]{1,0:T(8,128)}, f32[1,128]{1,0:T(1,128)}) custom-call(bf16[128,2880]{1,0:T(8,128)(2,1)} %bitcast.4, f32[1,2880]{1,0:T(1,128)} %reshape.9.gain_hbm, bf16[2880,2048]{1,0:T(8,128)(2,1)} %qw_hbm.1, bf16[2880,512]{1,0:T(8,128)(2,1)} %kvw_hbm.1, f32[32]{0:T(128)} %sink_ref.1, s32[1,128]{1,0:T(1,128)} %docs_ref.1, ...), custom_call_target="tpu_custom_call" | custom-call | tf_op jit(solution)/shard_map/attention_step/pallas_call | solution.py:332
  58.6 1.9 %copy.16 = bf16[1,128,2048]{2,1,0:T(8,128)(2,1)} copy(bf16[1,128,2048]{2,1,0:T(8,128)(2,1)} %bitcast.5) | data formatting | bytes 1048576
  60.5 1.3 %copy.17 = f32[1,32,128]{2,1,0:T(8,128)} copy(f32[1,32,128]{2,1,0:T(8,128)} %bitcast.6) | data formatting | bytes 32768
  61.8 1.1 %copy.18 = f32[1,128]{1,0:T(1,128)} copy(f32[1,128]{1,0:T(1,128)} %get-tuple-element.14) | data formatting | bytes 1024

commit v2 on v1

v2 whole, which is shorter than its diff:
```python
import functools
import math

import jax
import jax.numpy as jnp
import numpy as np
from jax import lax
from jax.experimental import pallas as pl
from jax.experimental.pallas import tpu as pltpu
from jax.sharding import PartitionSpec as P

MESH = pl.DeviceIdType.MESH
HEAD_DIM = 64
DOC_MOST = 1024
ROPE_BASE = 150000.0
NORM_EPS = 1e-05
MASKED = -1e30
LOG2E = 1.4426950408889634
LN2 = 0.6931471805599453
F32 = jnp.float32
BF16 = jnp.bfloat16
NT = (((1,), (1,)), ((), ()))
Q_CHUNK = 512
HEADS_STEP = 4
DOC_AT = 1


def iota(shape, dim):
    return lax.broadcasted_iota(jnp.int32, shape, dim)


def exact_dot(a, b, dims=(((1,), (0,)), ((), ()))):
    return lax.dot_general(a, b, dims, precision=lax.Precision.HIGHEST, preferred_element_type=F32)


def cos_sin(angle):
    k = jnp.floor(angle * (2.0 / math.pi) + 0.5)
    r = ((angle - k * 1.5703125) - k * 4.837512969970703125e-4) - k * 7.549789954891882e-8
    z = r * r
    s = ((-1.9515295891e-4 * z + 8.3321608736e-3) * z - 1.6666654611e-1) * z * r + r
    c = ((2.443315711809948e-5 * z - 1.388731625493765e-3) * z + 4.166664568298827e-2) * z * z - 0.5 * z + 1.0
    q = k.astype(jnp.int32) & 3
    odd = (q & 1) == 1
    cosine = jnp.where(odd, s, c)
    sine = jnp.where(odd, c, s)
    cosine = jnp.where((q == 1) | (q == 2), -cosine, cosine)
    sine = jnp.where(q >= 2, -sine, sine)
    return cosine, sine


def kernel(
    shape,
    groups,
    hidden_hbm, gain_hbm, qw_hbm, kvw_hbm, sink_hbm, docs_hbm, owner_hbm, mask_hbm, freq_hbm,
    att_hbm, lse_hbm, tw_hbm,
    hid, gain, kvw, qw, normed, qt, qz, kbuf, vbuf, bias,
    docs_buf, cnt_send, cnt_buf, m_ref, acc_ref, lse_ref, comb_send, comb, s_even, s_odd, top_even, top_odd,
    sink_ref, owner_ref, mask_ref, freq_ref, att_ref, lse_out_ref, tw_ref,
    load_sem, qw_sem,
    doc_ssem, doc_rsem, kv_ssem, kv_rsem, cnt_ssem, cnt_rsem, lse_ssem, lse_rsem,
):
    rows, width, heads, kv_heads, shards, dps = shape
    back = DOC_MOST // rows
    per_kv = heads // kv_heads
    block_rows = rows // shards
    me = lax.axis_index("cp")
    my_dp = lax.axis_index("dp")
    qdim = heads * HEAD_DIM
    n_chunks = qdim // Q_CHUNK
    pairs = heads // HEADS_STEP
    half = HEAD_DIM // 2

    def ahead(k):
        return lax.rem(me + k, shards)

    loads = [
        pltpu.make_async_copy(hidden_hbm, hid, load_sem.at[0]),
        pltpu.make_async_copy(gain_hbm, gain, load_sem.at[1]),
        pltpu.make_async_copy(docs_hbm, docs_buf.at[back], load_sem.at[2]),
        pltpu.make_async_copy(mask_hbm, mask_ref, load_sem.at[3]),
        pltpu.make_async_copy(kvw_hbm, kvw, load_sem.at[4]),
        pltpu.make_async_copy(freq_hbm, freq_ref, load_sem.at[5]),
        pltpu.make_async_copy(sink_hbm, sink_ref, load_sem.at[6]),
        pltpu.make_async_copy(owner_hbm, owner_ref, load_sem.at[7]),
    ]
    for c in loads:
        c.start()

    barrier = pltpu.get_barrier_semaphore()

    def greet(k, carry):
        pl.semaphore_signal(barrier, inc=1, device_id={"cp": ahead(k)}, device_id_type=MESH)
        return carry

    lax.fori_loop(1, shards, greet, 0)
    for k in range(1, dps):
        pl.semaphore_signal(
            barrier, inc=1, device_id={"dp": lax.rem(my_dp + k, dps)}, device_id_type=MESH
        )

    loads[0].wait()
    loads[1].wait()
    q_loads = [
        pltpu.make_async_copy(qw_hbm.at[:, pl.ds(i * Q_CHUNK, Q_CHUNK)], qw.at[i], qw_sem.at[i])
        for i in range(n_chunks)
    ]
    for c in q_loads:
        c.start()
    loads[2].wait()
    loads[3].wait()
    own_docs = docs_buf[back]
    flags = mask_ref[...].astype(F32)
    cnt_row = jnp.broadcast_to(jnp.sum(flags, axis=1, keepdims=True), (1, rows))
    cnt_send[0] = cnt_row
    cnt_buf[0] = cnt_row
    x = hid[...].T.astype(F32)
    inv = lax.rsqrt(jnp.sum(x * x, axis=1, keepdims=True) * (1.0 / width) + NORM_EPS)
    normed[...] = (x * inv * gain[...].reshape(1, width)).astype(BF16)

    pl.semaphore_wait(barrier, shards - 1 + dps - 1)

    sends = []

    def send(src, dst, ssem, rsem, device):
        c = pltpu.make_async_remote_copy(
            src_ref=src, dst_ref=dst, send_sem=ssem, recv_sem=rsem,
            device_id=device, device_id_type=MESH,
        )
        c.start()
        sends.append(c)
        return c

    doc_copies = {}
    for k in range(1, back + 1):
        doc_copies[k] = send(
            docs_buf.at[back], docs_buf.at[back - k], doc_ssem.at[k - 1], doc_rsem.at[k - 1],
            {"cp": ahead(k)},
        )
    cnt_copies = []
    for k in range(1, dps):
        cnt_copies.append(send(
            cnt_send.at[0], cnt_buf.at[k], cnt_ssem.at[k - 1], cnt_rsem.at[k - 1],
            {"dp": lax.rem(my_dp + k, dps)},
        ))

    core = lax.rem(me, 2)
    chips = back // 2
    z = lax.rem(me // 2, chips)
    corner = me - 2 * z
    bufs = (vbuf, kbuf)

    def slot_copy(t, src, dst, sem, device):
        buf = bufs[t]
        return pltpu.make_async_remote_copy(
            src_ref=buf.at[src], dst_ref=buf.at[dst], send_sem=kv_ssem.at[t, sem],
            recv_sem=kv_rsem.at[t, dst], device_id={"cp": device}, device_id_type=MESH,
        )

    def row_copy(t, k, src):
        return slot_copy(t, src, back - 2 * k, k, corner + 2 * lax.rem(z + k, chips))

    def next_row_copy(t):
        return slot_copy(t, back, 0, 0, ahead(back))

    def partner_copy(t, src, dst):
        return slot_copy(t, src, dst, chips + src // 2 if src != back else chips, me + 1 - 2 * core)

    def send_own(t):
        @pl.when(core == 0)
        def _():
            partner_copy(t, back, back - 1).start()

        next_row_copy(t).start()
        for k in range(1, chips):
            @pl.when(z + k < chips)
            def _(k=k):
                row_copy(t, k, back).start()

    def arrived(t, slot):
        slot_copy(t, slot, slot, 0, me).wait_recv()

    def serve(t, slot):
        arrived(t, slot)
        if slot == 0:
            for k in range(1, chips):
                @pl.when(z + k >= chips)
                def _(k=k):
                    row_copy(t, k, 0).start()

            @pl.when(core == 1)
            def _():
                partner_copy(t, 0, 1).start()
        else:
            partner_copy(t, slot, slot - 1 + 2 * core).start()

    loads[4].wait()
    kv = jnp.dot(normed[...], kvw[...], preferred_element_type=F32)
    kv_width = kv_heads * HEAD_DIM
    raw_kt = []
    for t in range(kv_heads // 2):
        v_t = kv[:, kv_width + t * 128:kv_width + (t + 1) * 128].T.astype(BF16)
        vbuf[back, 2 * t] = v_t[:HEAD_DIM]
        vbuf[back, 2 * t + 1] = v_t[HEAD_DIM:]
        raw_kt.append(kv[:, t * 128:(t + 1) * 128].T)

    def q_part(i):
        q_loads[i].wait()
        part = jnp.dot(normed[...], qw[i], preferred_element_type=F32)
        for t in range(Q_CHUNK // 128):
            at = i * Q_CHUNK + t * 128
            qt[at:at + 128] = part[:, t * 128:(t + 1) * 128].T

    send_own(0)

    for i in range(DOC_AT):
        q_part(i)

    for k in range(1, back + 1):
        doc_copies[k].wait_recv()
    for i in range(5, 8):
        loads[i].wait()
    square = (rows, 128)
    lane = iota(square, 1)
    sub = iota(square, 0)
    own_row = jnp.broadcast_to(own_docs.astype(F32), square)
    own_col = own_row.T
    count = jnp.zeros(square, F32)
    for b in range(back + 1):
        window_docs = docs_buf[b].astype(F32)
        if b < back:
            window_docs = jnp.where(me >= back - b, window_docs, -1.0)
        count = count + (jnp.broadcast_to(window_docs, square) < own_col).astype(F32)
    start_row = jnp.broadcast_to(jnp.sum(count, axis=1, keepdims=True), square).T
    within = (lane[:half] + back * rows).astype(F32) - start_row[:half]
    cosine, sine = cos_sin(within * freq_ref[...])

    def rope(u):
        a, b = u[:half], u[half:]
        return jnp.concatenate([a * cosine - b * sine, b * cosine + a * sine], axis=0)

    for t in range(kv_heads // 2):
        u = raw_kt[t]
        u = jnp.concatenate([rope(u[:HEAD_DIM]), rope(u[HEAD_DIM:])], axis=0)
        kbuf[back, t] = u.T.astype(BF16)
    send_own(1)

    serve(0, 0)
    for i in range(DOC_AT, 3):
        q_part(i)
    serve(1, 0)
    for i in range(3, n_chunks):
        q_part(i)

    scale = HEAD_DIM ** (-0.5)
    zeros = jnp.zeros((HEAD_DIM, rows), BF16)
    for h in range(heads):
        y = (rope(qt[h * HEAD_DIM:(h + 1) * HEAD_DIM]) * scale).astype(BF16)
        at = (h // per_kv) % 2
        lanes = slice((h % HEADS_STEP) * rows, (h % HEADS_STEP + 1) * rows)
        qz[h // HEADS_STEP, at * HEAD_DIM:(at + 1) * HEAD_DIM, lanes] = y
        qz[h // HEADS_STEP, (1 - at) * HEAD_DIM:(2 - at) * HEAD_DIM, lanes] = zeros

    for b in range(back + 1):
        place = (sub + b * rows).astype(F32)
        allowed = place >= start_row
        if b == back:
            allowed = allowed & (sub <= lane)
        bias[b] = jnp.where(allowed, 0.0, MASKED)

    serve(0, 6)
    serve(1, 6)
    serve(0, 4)
    serve(1, 4)
    serve(0, 2)
    serve(1, 2)
    arrived(0, 7)
    arrived(1, 7)
    arrived(0, 5)
    arrived(1, 5)
    arrived(0, 3)
    arrived(1, 3)
    arrived(0, 1)
    arrived(1, 1)
    two = HEADS_STEP * rows
    head_lane = iota((1, two), 1) // rows
    acc_rows = HEAD_DIM + 16
    for gi, (b0, b1) in enumerate(groups):
        first, last = gi == 0, gi == len(groups) - 1
        nb = b1 - b0
        ones_rows = jnp.ones((16, nb * rows), BF16)

        def score(j, s_ref, t_ref, b0=b0, b1=b1, nb=nb):
            a = j // (per_kv // HEADS_STEP)
            kb = jnp.concatenate([kbuf[b, a // 2] for b in range(b0, b1)], axis=0)
            s = jnp.dot(kb, qz[j], preferred_element_type=F32)
            top = None
            for b in range(nb):
                bb = bias[b0 + b]
                sb = s[b * rows:(b + 1) * rows] * LOG2E + jnp.concatenate([bb] * HEADS_STEP, axis=1)
                s_ref[b * rows:(b + 1) * rows] = sb
                part = jnp.max(sb.reshape(rows // 8, 8, two), axis=0)
                top = part if top is None else jnp.maximum(top, part)
            t_ref[...] = top

        def mix(j, s_ref, t_ref, b0=b0, b1=b1, nb=nb, first=first, last=last, ones_rows=ones_rows):
            a = j // (per_kv // HEADS_STEP)
            top = jnp.max(t_ref[...], axis=0, keepdims=True)
            if first:
                old = jnp.zeros((1, two), F32)
                for i in range(HEADS_STEP):
                    old = jnp.where(head_lane == i, sink_ref[HEADS_STEP * j + i] * LOG2E, old)
            else:
                old = m_ref[j][:1]
            new = jnp.maximum(old, top)
            weights = jnp.exp2(s_ref[:nb * rows] - new).astype(BF16)
            vt = jnp.concatenate([vbuf[b, a] for b in range(b0, b1)], axis=1)
            vt = jnp.concatenate([vt, ones_rows], axis=0)
            mixed = jnp.dot(vt, weights, preferred_element_type=F32)
            shrink = jnp.exp2(old - new)
            if first:
                acc = mixed + jnp.where(iota((acc_rows, two), 0) >= HEAD_DIM, shrink, 0.0)
            else:
                acc = acc_ref[j] * shrink + mixed
            if last:
                total = acc[HEAD_DIM:HEAD_DIM + 1]
                out = acc[:HEAD_DIM] * (1.0 / total)
                lse = (new + jnp.log2(total)) * LN2
                for i in range(0, HEADS_STEP, 2):
                    both = jnp.concatenate([out[:, i * rows:(i + 1) * rows], out[:, (i + 1) * rows:(i + 2) * rows]], axis=0).T
                    at = pl.multiple_of(j * (HEADS_STEP * HEAD_DIM) + i * HEAD_DIM, 128)
                    att_ref[:, pl.ds(at, 128)] = both.astype(BF16)
                for i in range(HEADS_STEP):
                    lse_ref[pl.ds(HEADS_STEP * j + i, 1), :] = lse[:, i * rows:(i + 1) * rows]
            else:
                acc_ref[j] = acc
                m_ref[j] = jnp.broadcast_to(new, (8, two))

        def two_pairs(i, carry, score=score, mix=mix):
            j = 2 * i
            score(j + 1, s_odd, top_odd)
            mix(j, s_even, top_even)
            score(lax.rem(j + 2, pairs), s_even, top_even)
            mix(j + 1, s_odd, top_odd)
            return carry

        with jax.named_scope("loop%d" % gi):
            score(0, s_even, top_even)
            lax.fori_loop(0, pairs // 2, two_pairs, 0)

    att_copy = pltpu.make_async_copy(att_ref, att_hbm, load_sem.at[0])
    att_copy.start()
    for c in cnt_copies:
        c.wait_recv()
    cnt = cnt_buf[0]
    for k in range(1, dps):
        cnt = cnt + cnt_buf[k]

    spread = (iota((shards, rows), 1) // block_rows == iota((shards, rows), 0)).astype(F32)
    owner_row = jnp.broadcast_to(owner_ref[...].astype(F32), (8, shards))
    owner_wide = exact_dot(owner_row, spread)[:1]
    chosen = (jnp.broadcast_to(owner_wide, (shards, rows)) == iota((shards, rows), 0).astype(F32)).astype(F32)
    wide = block_rows * heads
    lse4 = jnp.concatenate([lse_ref[...]] * block_rows, axis=0)
    lse4 = jnp.where(iota((wide, rows), 1) % block_rows == iota((wide, rows), 0) // heads, lse4, 0.0)
    rows_out = exact_dot(chosen, lse4, NT)
    comb_send[:, 0, :] = rows_out
    comb_send[:, 1, :] = jnp.broadcast_to(cnt, (shards, rows))
    comb[me] = comb_send[me]

    def lse_copy(k):
        return pltpu.make_async_remote_copy(
            src_ref=comb_send.at[ahead(k)], dst_ref=comb.at[me],
            send_sem=lse_ssem.at[k], recv_sem=lse_rsem.at[k],
            device_id={"cp": ahead(k)}, device_id_type=MESH,
        )

    def lse_send(k, carry):
        lse_copy(k).start()
        return carry

    def lse_wait(k, carry):
        lse_copy(k).wait_recv()
        return carry

    def lse_done(k, carry):
        lse_copy(k).wait_send()
        return carry

    lax.fori_loop(1, shards, lse_send, 0)
    lax.fori_loop(1, shards, lse_wait, 0)

    got = comb[:, 0, :]
    totals = jnp.sum(comb[:, 1, :], axis=0, keepdims=True)
    back_spread = (iota((rows, shards), 0) // block_rows == iota((rows, shards), 1)).astype(F32)
    wide_got = exact_dot(back_spread, got)
    wide_got = jnp.where(iota((rows, wide), 0) % block_rows == iota((rows, wide), 1) // heads, wide_got, 0.0)
    pick = (iota((heads, wide), 1) % heads == iota((heads, wide), 0)).astype(F32)
    lse_out_ref[...] = exact_dot(pick, wide_got, NT)
    lse_move = pltpu.make_async_copy(lse_out_ref, lse_hbm, load_sem.at[1])
    lse_move.start()
    tw_ref[...] = flags * (float(dps * shards * rows) / totals)
    tw_move = pltpu.make_async_copy(tw_ref, tw_hbm, load_sem.at[2])
    tw_move.start()

    att_copy.wait()
    lse_move.wait()
    tw_move.wait()
    for c in sends:
        c.wait_send()
    for t in range(2):
        for sem in range(2 * chips):
            slot_copy(t, back, 0, sem, me).wait_send()
    lax.fori_loop(1, shards, lse_done, 0)


def store(att_in, lse_in, tw_in, att_out, lse_out, tw_out, att, lse, tw, in_sem, out_sem):
    parts = 4
    step = att.shape[0] // parts
    moves = [(att_in.at[pl.ds(i * step, step)], att.at[pl.ds(i * step, step)], att_out.at[pl.ds(i * step, step)]) for i in range(parts)]
    moves += [(lse_in, lse, lse_out), (tw_in, tw, tw_out)]
    ins = [pltpu.make_async_copy(a, b, in_sem.at[i]) for i, (a, b, c) in enumerate(moves)]
    outs = [pltpu.make_async_copy(b, c, out_sem.at[i]) for i, (a, b, c) in enumerate(moves)]
    for c in ins:
        c.start()
    for i, c in enumerate(outs):
        ins[i].wait()
        c.start()
    for c in outs:
        c.wait()


def solution(mesh):
    dps, shards = mesh.shape["dp"], mesh.shape["cp"]
    half = HEAD_DIM // 2
    freq_np = np.broadcast_to(ROPE_BASE ** (-np.arange(half).astype(np.float64) / half)[:, None], (half, 128))

    def body(hidden, norm_gain, query_weight, keyval_weight, sink_logits, document_ids, block_owner, loss_mask):
        rows, width = hidden.shape[1:]
        heads = sink_logits.shape[0]
        kv_heads = keyval_weight.shape[1] // (2 * HEAD_DIM)
        qdim = heads * HEAD_DIM
        back = DOC_MOST // rows
        slots = back + 1
        pairs = heads // HEADS_STEP
        groups = ((back - 2, back + 1), (back - 5, back - 2), (0, back - 5))
        widest = max(b1 - b0 for b0, b1 in groups) * rows
        shape = (rows, width, heads, kv_heads, shards, dps)
        hbm = pl.BlockSpec(memory_space=pltpu.HBM)
        dma = pltpu.SemaphoreType.DMA
        att, lse, tw = pl.pallas_call(
            functools.partial(kernel, shape, groups),
            name="attention_step",
            out_shape=(
                jax.ShapeDtypeStruct((rows, qdim), BF16),
                jax.ShapeDtypeStruct((heads, rows), F32),
                jax.ShapeDtypeStruct((1, rows), F32),
            ),
            in_specs=[hbm] * 9,
            out_specs=(hbm, hbm, hbm),
            scratch_shapes=[
                pltpu.VMEM((width, rows), BF16),
                pltpu.VMEM((width,), F32),
                pltpu.VMEM((width, keyval_weight.shape[1]), BF16),
                pltpu.VMEM((qdim // Q_CHUNK, width, Q_CHUNK), BF16),
                pltpu.VMEM((rows, width), BF16),
                pltpu.VMEM((qdim, rows), F32),
                pltpu.VMEM((pairs, 128, HEADS_STEP * rows), BF16),
                pltpu.VMEM((slots, kv_heads // 2, rows, 128), BF16),
                pltpu.VMEM((slots, kv_heads, HEAD_DIM, rows), BF16),
                pltpu.VMEM((slots, rows, rows), F32),
                pltpu.VMEM((slots, 1, rows), jnp.int32),
                pltpu.VMEM((1, 1, rows), F32),
                pltpu.VMEM((dps, 1, rows), F32),
                pltpu.VMEM((pairs, 8, HEADS_STEP * rows), F32),
                pltpu.VMEM((pairs, HEAD_DIM + 16, HEADS_STEP * rows), F32),
                pltpu.VMEM((heads, rows), F32),
                pltpu.VMEM((shards, 2, rows), F32),
                pltpu.VMEM((shards, 2, rows), F32),
                pltpu.VMEM((widest, HEADS_STEP * rows), F32),
                pltpu.VMEM((widest, HEADS_STEP * rows), F32),
                pltpu.VMEM((8, HEADS_STEP * rows), F32),
                pltpu.VMEM((8, HEADS_STEP * rows), F32),
                pltpu.SMEM((heads,), F32),
                pltpu.VMEM((1, shards), jnp.int32),
                pltpu.VMEM((1, rows), jnp.int32),
                pltpu.VMEM((half, 128), F32),
                pltpu.VMEM((rows, qdim), BF16),
                pltpu.VMEM((heads, rows), F32),
                pltpu.VMEM((1, rows), F32),
                dma((8,)), dma((qdim // Q_CHUNK,)),
                dma((back,)), dma((back,)),
                dma((2, back)), dma((2, back)),
                dma((dps,)), dma((dps,)),
                dma((shards,)), dma((shards,)),
            ],
            compiler_params=pltpu.CompilerParams(
                collective_id=0, has_side_effects=True, vmem_limit_bytes=58 * 1024 * 1024
            ),
        )(
            hidden[0].T, norm_gain, query_weight, keyval_weight, sink_logits,
            document_ids, block_owner[0], loss_mask,
            jnp.asarray(freq_np, F32),
        )
        results = (att, lse, tw)
        att, lse, tw = pl.pallas_call(
            store,
            name="store_results",
            out_shape=tuple(jax.ShapeDtypeStruct(r.shape, r.dtype) for r in results),
            in_specs=[hbm] * 3,
            out_specs=(hbm,) * 3,
            scratch_shapes=[pltpu.VMEM(r.shape, r.dtype) for r in results] + [dma((6,)), dma((6,))],
            compiler_params=pltpu.CompilerParams(vmem_limit_bytes=58 * 1024 * 1024),
        )(*results)
        return att[None], lse[None], tw

    return jax.shard_map(
        body,
        mesh=mesh,
        in_specs=(
            P("dp", "cp", None), P(), P(), P(), P(), P("dp", "cp"), P("dp", "cp", None), P("dp", "cp"),
        ),
        out_specs=(P("dp", "cp", None), P("dp", None, "cp"), P("dp", "cp")),
        check_vma=False,
    )
```

time: 63.3 us -> 38.4 us (0.61)
  Pallas kernels: 54.4 us -> 37.6 us
  local copies, waits for them, and re-layouts: 7.92 us -> 0 us
    pallas_call x1, Pallas kernels: 54.4 us -> 35.7 us  [body(): pl.pallas_call(functools.partial(kernel, shape, groups), name='attention_...]
    unnamed x4 -> x0, local copies, waits for them, and re-layouts: 6.6 us -> none
    pallas_call x0 -> x1, Pallas kernels: none -> 1.86 us  [body(): pl.pallas_call(store, name='store_results', out_shape=tuple((jax.ShapeDty...]
    reshape x1 -> x0, local copies, waits for them, and re-layouts: 1.32 us -> none  [body(): norm_gain.reshape(1, width)]
where the time goes in v2:
time: 38.4 us; the launch traced here: 38.2 us
  Pallas kernels  37.6 us (98%)
  between operations  0.64 us (2%)
    pallas_call x1, Pallas kernels, body(): pl.pallas_call(functools.partial(kernel, shape, groups), name='attention_...  35.7 us
    pallas_call x1, Pallas kernels, body(): pl.pallas_call(store, name='store_results', out_shape=tuple((jax.ShapeDty...  1.86 us

profile of v2, /device:TPU:1, one launch (start us, length us, event | category | flops | bytes accessed | tf_op | source)
XLA Modules:
  0.0 38.2 jit_solution(14191016078794461676)
XLA Ops:
  0.6 35.7 %attention_step.1 = (bf16[128,2048]{1,0:T(8,128)(2,1)}, f32[32,128]{1,0:T(8,128)}, f32[1,128]{1,0:T(1,128)}) custom-call(bf16[2880,128]{1,0:T(8,128)(2,1)} %bitcast.6, f32[2880]{0:T(1024)} %gain_hbm.1, bf16[2880,2048]{1,0:T(8,128)(2,1)} %qw_hbm.1, bf16[2880,512]{1,0:T(8,128)(2,1)} %kvw_hbm.1, f32[32]{0:T(128)} %sink_hbm.1, s32[1,128]{1,0:T(1,128)} %docs_hbm.1, ...), custom_call_target="tpu_custom_call" | custom-call | tf_op jit(solution)/shard_map/attention_step/pallas_call | solution.py:450
  36.4 1.9 %store_results.1 = (bf16[128,2048]{1,0:T(8,128)(2,1)}, f32[32,128]{1,0:T(8,128)}, f32[1,128]{1,0:T(1,128)}) custom-call(bf16[128,2048]{1,0:T(8,128)(2,1)} %get-tuple-element.9.att_in, f32[32,128]{1,0:T(8,128)} %get-tuple-element.10.lse_in, f32[1,128]{1,0:T(1,128)} %get-tuple-element.11.tw_in), custom_call_target="tpu_custom_call" | custom-call | tf_op jit(solution)/shard_map/store_results/pallas_call | solution.py:505

commit v3 on v2

--- a/solution.py
+++ b/solution.py
@@ -22,7 +22,7 @@
 NT = (((1,), (1,)), ((), ()))
 Q_CHUNK = 512
 HEADS_STEP = 4
-DOC_AT = 1
+DOC_AT = 2
 
 
 def iota(shape, dim):
@@ -50,14 +50,13 @@
 
 def kernel(
     shape,
-    groups,
     hidden_hbm, gain_hbm, qw_hbm, kvw_hbm, sink_hbm, docs_hbm, owner_hbm, mask_hbm, freq_hbm,
     att_hbm, lse_hbm, tw_hbm,
     hid, gain, kvw, qw, normed, qt, qz, kbuf, vbuf, bias,
     docs_buf, cnt_send, cnt_buf, m_ref, acc_ref, lse_ref, comb_send, comb, s_even, s_odd, top_even, top_odd,
-    sink_ref, owner_ref, mask_ref, freq_ref, att_ref, lse_out_ref, tw_ref,
+    chosen3, sink_ref, owner_ref, mask_ref, freq_ref, att_ref, lse_out_ref, tw_ref,
     load_sem, qw_sem,
-    doc_ssem, doc_rsem, kv_ssem, kv_rsem, cnt_ssem, cnt_rsem, lse_ssem, lse_rsem,
+    doc_sem, kv_ssem, kv_rsem, cnt_ssem, cnt_rsem, lse_sem,
 ):
     rows, width, heads, kv_heads, shards, dps = shape
     back = DOC_MOST // rows
@@ -88,11 +87,9 @@
 
     barrier = pltpu.get_barrier_semaphore()
 
-    def greet(k, carry):
-        pl.semaphore_signal(barrier, inc=1, device_id={"cp": ahead(k)}, device_id_type=MESH)
-        return carry
-
-    lax.fori_loop(1, shards, greet, 0)
+    for k in range(1, back + 1):
+        for at in (k, shards - k):
+            pl.semaphore_signal(barrier, inc=1, device_id={"cp": ahead(at)}, device_id_type=MESH)
     for k in range(1, dps):
         pl.semaphore_signal(
             barrier, inc=1, device_id={"dp": lax.rem(my_dp + k, dps)}, device_id_type=MESH
@@ -117,25 +114,22 @@
     inv = lax.rsqrt(jnp.sum(x * x, axis=1, keepdims=True) * (1.0 / width) + NORM_EPS)
     normed[...] = (x * inv * gain[...].reshape(1, width)).astype(BF16)
 
-    pl.semaphore_wait(barrier, shards - 1 + dps - 1)
+    pl.semaphore_wait(barrier, 2 * back + dps - 1)
 
     sends = []
 
-    def send(src, dst, ssem, rsem, device):
+    def send(src, dst, ssem, rsem, device, keep=True):
         c = pltpu.make_async_remote_copy(
             src_ref=src, dst_ref=dst, send_sem=ssem, recv_sem=rsem,
             device_id=device, device_id_type=MESH,
         )
         c.start()
-        sends.append(c)
+        if keep:
+            sends.append(c)
         return c
 
-    doc_copies = {}
     for k in range(1, back + 1):
-        doc_copies[k] = send(
-            docs_buf.at[back], docs_buf.at[back - k], doc_ssem.at[k - 1], doc_rsem.at[k - 1],
-            {"cp": ahead(k)},
-        )
+        send(docs_buf.at[back], docs_buf.at[back - k], doc_sem.at[0], doc_sem.at[1], {"cp": ahead(k)}, False)
     cnt_copies = []
     for k in range(1, dps):
         cnt_copies.append(send(
@@ -212,13 +206,26 @@
 
     send_own(0)
 
+    def docs_all():
+        part = docs_buf.at[pl.ds(0, back)]
+        return pltpu.make_async_remote_copy(
+            src_ref=part, dst_ref=part, send_sem=doc_sem.at[0], recv_sem=doc_sem.at[1],
+            device_id={"cp": me}, device_id_type=MESH,
+        )
+
     for i in range(DOC_AT):
         q_part(i)
 
-    for k in range(1, back + 1):
-        doc_copies[k].wait_recv()
     for i in range(5, 8):
         loads[i].wait()
+    spread = (iota((shards, rows), 1) // block_rows == iota((shards, rows), 0)).astype(F32)
+    owner_row = jnp.broadcast_to(owner_ref[...].astype(F32), (8, shards))
+    owner_wide = exact_dot(owner_row, spread)[:1]
+    chosen = jnp.broadcast_to(owner_wide, (shards, rows)) == iota((shards, rows), 0).astype(F32)
+    chosen = chosen.astype(F32).astype(BF16)
+    chosen3[...] = jnp.concatenate([chosen] * 3, axis=1)
+
+    docs_all().wait_recv()
     square = (rows, 128)
     lane = iota(square, 1)
     sub = iota(square, 0)
@@ -244,13 +251,10 @@
         kbuf[back, t] = u.T.astype(BF16)
     send_own(1)
 
+    for i in range(DOC_AT, n_chunks):
+        q_part(i)
+
     serve(0, 0)
-    for i in range(DOC_AT, 3):
-        q_part(i)
-    serve(1, 0)
-    for i in range(3, n_chunks):
-        q_part(i)
-
     scale = HEAD_DIM ** (-0.5)
     zeros = jnp.zeros((HEAD_DIM, rows), BF16)
     for h in range(heads):
@@ -267,42 +271,53 @@
             allowed = allowed & (sub <= lane)
         bias[b] = jnp.where(allowed, 0.0, MASKED)
 
-    serve(0, 6)
-    serve(1, 6)
-    serve(0, 4)
-    serve(1, 4)
-    serve(0, 2)
-    serve(1, 2)
-    arrived(0, 7)
-    arrived(1, 7)
-    arrived(0, 5)
-    arrived(1, 5)
-    arrived(0, 3)
-    arrived(1, 3)
-    arrived(0, 1)
-    arrived(1, 1)
+    serve(1, 0)
+    extra = 1 + 6 * core
+    odds = tuple(b + 1 - 2 * core for b in (6, 4, 2))
+
+    def before_0():
+        arrived(0, extra)
+        arrived(1, extra)
+
+    def before_1():
+        for slot in (6, 4, 2):
+            serve(0, slot)
+            serve(1, slot)
+
+    def before_2():
+        for slot in odds:
+            arrived(0, slot)
+            arrived(1, slot)
+
+    groups = (
+        (before_0, (back, 0, extra)),
+        (before_1, (6, 4, 2)),
+        (before_2, odds),
+    )
     two = HEADS_STEP * rows
     head_lane = iota((1, two), 1) // rows
     acc_rows = HEAD_DIM + 16
-    for gi, (b0, b1) in enumerate(groups):
+    for gi, (before, slots) in enumerate(groups):
+        with jax.named_scope("before%d" % gi):
+            before()
         first, last = gi == 0, gi == len(groups) - 1
-        nb = b1 - b0
+        nb = len(slots)
         ones_rows = jnp.ones((16, nb * rows), BF16)
 
-        def score(j, s_ref, t_ref, b0=b0, b1=b1, nb=nb):
+        def score(j, s_ref, t_ref, slots=slots, nb=nb):
             a = j // (per_kv // HEADS_STEP)
-            kb = jnp.concatenate([kbuf[b, a // 2] for b in range(b0, b1)], axis=0)
+            kb = jnp.concatenate([kbuf[b, a // 2] for b in slots], axis=0)
             s = jnp.dot(kb, qz[j], preferred_element_type=F32)
             top = None
             for b in range(nb):
-                bb = bias[b0 + b]
+                bb = bias[slots[b]]
                 sb = s[b * rows:(b + 1) * rows] * LOG2E + jnp.concatenate([bb] * HEADS_STEP, axis=1)
                 s_ref[b * rows:(b + 1) * rows] = sb
                 part = jnp.max(sb.reshape(rows // 8, 8, two), axis=0)
                 top = part if top is None else jnp.maximum(top, part)
             t_ref[...] = top
 
-        def mix(j, s_ref, t_ref, b0=b0, b1=b1, nb=nb, first=first, last=last, ones_rows=ones_rows):
+        def mix(j, s_ref, t_ref, slots=slots, nb=nb, first=first, last=last, ones_rows=ones_rows):
             a = j // (per_kv // HEADS_STEP)
             top = jnp.max(t_ref[...], axis=0, keepdims=True)
             if first:
@@ -312,10 +327,15 @@
             else:
                 old = m_ref[j][:1]
             new = jnp.maximum(old, top)
-            weights = jnp.exp2(s_ref[:nb * rows] - new).astype(BF16)
-            vt = jnp.concatenate([vbuf[b, a] for b in range(b0, b1)], axis=1)
-            vt = jnp.concatenate([vt, ones_rows], axis=0)
-            mixed = jnp.dot(vt, weights, preferred_element_type=F32)
+            mixed = None
+            for b in range(0, nb, 2):
+                part = slots[b:b + 2]
+                n = len(part) * rows
+                weights = jnp.exp2(s_ref[b * rows:b * rows + n] - new).astype(BF16)
+                vt = jnp.concatenate([vbuf[i, a] for i in part], axis=1)
+                vt = jnp.concatenate([vt, ones_rows[:, :n]], axis=0)
+                more = jnp.dot(vt, weights, preferred_element_type=F32)
+                mixed = more if mixed is None else mixed + more
             shrink = jnp.exp2(old - new)
             if first:
                 acc = mixed + jnp.where(iota((acc_rows, two), 0) >= HEAD_DIM, shrink, 0.0)
@@ -323,12 +343,8 @@
                 acc = acc_ref[j] * shrink + mixed
             if last:
                 total = acc[HEAD_DIM:HEAD_DIM + 1]
-                out = acc[:HEAD_DIM] * (1.0 / total)
+                acc_ref[j] = acc
                 lse = (new + jnp.log2(total)) * LN2
-                for i in range(0, HEADS_STEP, 2):
-                    both = jnp.concatenate([out[:, i * rows:(i + 1) * rows], out[:, (i + 1) * rows:(i + 2) * rows]], axis=0).T
-                    at = pl.multiple_of(j * (HEADS_STEP * HEAD_DIM) + i * HEAD_DIM, 128)
-                    att_ref[:, pl.ds(at, 128)] = both.astype(BF16)
                 for i in range(HEADS_STEP):
                     lse_ref[pl.ds(HEADS_STEP * j + i, 1), :] = lse[:, i * rows:(i + 1) * rows]
             else:
@@ -345,72 +361,86 @@
 
         with jax.named_scope("loop%d" % gi):
             score(0, s_even, top_even)
-            lax.fori_loop(0, pairs // 2, two_pairs, 0)
-
-    att_copy = pltpu.make_async_copy(att_ref, att_hbm, load_sem.at[0])
-    att_copy.start()
+            for j in range(0, pairs, 2):
+                score(j + 1, s_odd, top_odd)
+                mix(j, s_even, top_even)
+                if j + 2 < pairs:
+                    score(j + 2, s_even, top_even)
+                mix(j + 1, s_odd, top_odd)
+
     for c in cnt_copies:
         c.wait_recv()
     cnt = cnt_buf[0]
     for k in range(1, dps):
         cnt = cnt + cnt_buf[k]
 
-    spread = (iota((shards, rows), 1) // block_rows == iota((shards, rows), 0)).astype(F32)
-    owner_row = jnp.broadcast_to(owner_ref[...].astype(F32), (8, shards))
-    owner_wide = exact_dot(owner_row, spread)[:1]
-    chosen = (jnp.broadcast_to(owner_wide, (shards, rows)) == iota((shards, rows), 0).astype(F32)).astype(F32)
+    def pieces(v):
+        hi = v.astype(BF16)
+        rest = v - hi.astype(F32)
+        mid = rest.astype(BF16)
+        return [hi, mid, (rest - mid.astype(F32)).astype(BF16)]
+
     wide = block_rows * heads
     lse4 = jnp.concatenate([lse_ref[...]] * block_rows, axis=0)
     lse4 = jnp.where(iota((wide, rows), 1) % block_rows == iota((wide, rows), 0) // heads, lse4, 0.0)
-    rows_out = exact_dot(chosen, lse4, NT)
-    comb_send[:, 0, :] = rows_out
+    lse4 = jnp.concatenate(pieces(lse4), axis=1)
+    comb_send[:, 0, :] = lax.dot_general(chosen3[...], lse4, NT, preferred_element_type=F32)
     comb_send[:, 1, :] = jnp.broadcast_to(cnt, (shards, rows))
     comb[me] = comb_send[me]
 
-    def lse_copy(k):
+    def lse_send(k, carry):
+        pltpu.make_async_remote_copy(
+            src_ref=comb_send.at[ahead(k)], dst_ref=comb.at[me],
+            send_sem=lse_sem.at[0], recv_sem=lse_sem.at[1],
+            device_id={"cp": ahead(k)}, device_id_type=MESH,
+        ).start()
+        return carry
+
+    lax.fori_loop(1, shards, lse_send, 0, unroll=True)
+
+    for j in range(pairs):
+        acc = acc_ref[j]
+        out = acc[:HEAD_DIM] * (1.0 / acc[HEAD_DIM:HEAD_DIM + 1])
+        for i in range(0, HEADS_STEP, 2):
+            both = jnp.concatenate([out[:, i * rows:(i + 1) * rows], out[:, (i + 1) * rows:(i + 2) * rows]], axis=0).T
+            at = (j * HEADS_STEP + i) * HEAD_DIM
+            att_ref[:, at:at + 128] = both.astype(BF16)
+    att_copy = pltpu.make_async_copy(att_ref, att_hbm, load_sem.at[0])
+    att_copy.start()
+    def lse_all():
+        part = comb.at[pl.ds(0, shards - 1)]
         return pltpu.make_async_remote_copy(
-            src_ref=comb_send.at[ahead(k)], dst_ref=comb.at[me],
-            send_sem=lse_ssem.at[k], recv_sem=lse_rsem.at[k],
-            device_id={"cp": ahead(k)}, device_id_type=MESH,
+            src_ref=part, dst_ref=part, send_sem=lse_sem.at[0], recv_sem=lse_sem.at[1],
+            device_id={"cp": me}, device_id_type=MESH,
         )
 
-    def lse_send(k, carry):
-        lse_copy(k).start()
-        return carry
-
-    def lse_wait(k, carry):
-        lse_copy(k).wait_recv()
-        return carry
-
-    def lse_done(k, carry):
-        lse_copy(k).wait_send()
-        return carry
-
-    lax.fori_loop(1, shards, lse_send, 0)
-    lax.fori_loop(1, shards, lse_wait, 0)
-
-    got = comb[:, 0, :]
+    lse_all().wait_recv()
+
+    got = comb[:, 0, :].T
     totals = jnp.sum(comb[:, 1, :], axis=0, keepdims=True)
-    back_spread = (iota((rows, shards), 0) // block_rows == iota((rows, shards), 1)).astype(F32)
-    wide_got = exact_dot(back_spread, got)
-    wide_got = jnp.where(iota((rows, wide), 0) % block_rows == iota((rows, wide), 1) // heads, wide_got, 0.0)
-    pick = (iota((heads, wide), 1) % heads == iota((heads, wide), 0)).astype(F32)
-    lse_out_ref[...] = exact_dot(pick, wide_got, NT)
-    lse_move = pltpu.make_async_copy(lse_out_ref, lse_hbm, load_sem.at[1])
-    lse_move.start()
     tw_ref[...] = flags * (float(dps * shards * rows) / totals)
     tw_move = pltpu.make_async_copy(tw_ref, tw_hbm, load_sem.at[2])
     tw_move.start()
-
-    att_copy.wait()
-    lse_move.wait()
-    tw_move.wait()
+    placed = None
+    for r in range(block_rows):
+        part = jnp.concatenate(pieces(got[r * heads:(r + 1) * heads]), axis=0)
+        to = (iota((shards, rows), 1) == iota((shards, rows), 0) * block_rows + r).astype(F32).astype(BF16)
+        more = jnp.dot(part, to, preferred_element_type=F32)
+        placed = more if placed is None else placed + more
+    lse_out_ref[...] = placed[:heads] + placed[heads:2 * heads] + placed[2 * heads:]
+    lse_move = pltpu.make_async_copy(lse_out_ref, lse_hbm, load_sem.at[1])
+    lse_move.start()
+
     for c in sends:
         c.wait_send()
+    docs_all().wait_send()
     for t in range(2):
         for sem in range(2 * chips):
             slot_copy(t, back, 0, sem, me).wait_send()
-    lax.fori_loop(1, shards, lse_done, 0)
+    lse_all().wait_send()
+    att_copy.wait()
+    tw_move.wait()
+    lse_move.wait()
 
 
 def store(att_in, lse_in, tw_in, att_out, lse_out, tw_out, att, lse, tw, in_sem, out_sem):
@@ -442,13 +472,12 @@
         back = DOC_MOST // rows
         slots = back + 1
         pairs = heads // HEADS_STEP
-        groups = ((back - 2, back + 1), (back - 5, back - 2), (0, back - 5))
-        widest = max(b1 - b0 for b0, b1 in groups) * rows
+        widest = 3 * rows
         shape = (rows, width, heads, kv_heads, shards, dps)
         hbm = pl.BlockSpec(memory_space=pltpu.HBM)
         dma = pltpu.SemaphoreType.DMA
         att, lse, tw = pl.pallas_call(
-            functools.partial(kernel, shape, groups),
+            functools.partial(kernel, shape),
             name="attention_step",
             out_shape=(
                 jax.ShapeDtypeStruct((rows, qdim), BF16),
@@ -480,6 +509,7 @@
                 pltpu.VMEM((widest, HEADS_STEP * rows), F32),
                 pltpu.VMEM((8, HEADS_STEP * rows), F32),
                 pltpu.VMEM((8, HEADS_STEP * rows), F32),
+                pltpu.VMEM((shards, 3 * rows), BF16),
                 pltpu.SMEM((heads,), F32),
                 pltpu.VMEM((1, shards), jnp.int32),
                 pltpu.VMEM((1, rows), jnp.int32),
@@ -488,10 +518,10 @@
                 pltpu.VMEM((heads, rows), F32),
                 pltpu.VMEM((1, rows), F32),
                 dma((8,)), dma((qdim // Q_CHUNK,)),
-                dma((back,)), dma((back,)),
+                dma((2,)),
                 dma((2, back)), dma((2, back)),
-                dma((dps,)), dma((dps,)),
-                dma((shards,)), dma((shards,)),
+                dma((dps - 1,)), dma((dps - 1,)),
+                dma((2,)),
             ],
             compiler_params=pltpu.CompilerParams(
                 collective_id=0, has_side_effects=True, vmem_limit_bytes=58 * 1024 * 1024

time: 38.4 us -> 33 us (0.86)
  Pallas kernels: 37.6 us -> 32.3 us
    pallas_call x1, Pallas kernels: 35.7 us -> 30.4 us  [body(): pl.pallas_call(functools.partial(kernel, shape), name='attention_step', o...]
where the time goes in v3:
time: 33 us; the launch traced here: 32.9 us
  Pallas kernels  32.3 us (98%)
  between operations  0.64 us (2%)
    pallas_call x1, Pallas kernels, body(): pl.pallas_call(functools.partial(kernel, shape), name='attention_step', o...  30.4 us
    pallas_call x1, Pallas kernels, body(): pl.pallas_call(store, name='store_results', out_shape=tuple((jax.ShapeDty...  1.86 us

profile of v3, /device:TPU:1, one launch (start us, length us, event | category | flops | bytes accessed | tf_op | source)
XLA Modules:
  0.0 32.9 jit_solution(4346047654632305830)
XLA Ops:
  0.6 30.4 %attention_step.1 = (bf16[128,2048]{1,0:T(8,128)(2,1)}, f32[32,128]{1,0:T(8,128)}, f32[1,128]{1,0:T(1,128)}) custom-call(bf16[2880,128]{1,0:T(8,128)(2,1)} %bitcast.6, f32[2880]{0:T(1024)} %gain_hbm.1, bf16[2880,2048]{1,0:T(8,128)(2,1)} %qw_hbm.1, bf16[2880,512]{1,0:T(8,128)(2,1)} %kvw_hbm.1, f32[32]{0:T(128)} %sink_hbm.1, s32[1,128]{1,0:T(1,128)} %docs_hbm.1, ...), custom_call_target="tpu_custom_call" | custom-call | tf_op jit(solution)/shard_map/attention_step/pallas_call | solution.py:479
  31.0 1.9 %store_results.1 = (bf16[128,2048]{1,0:T(8,128)(2,1)}, f32[32,128]{1,0:T(8,128)}, f32[1,128]{1,0:T(1,128)}) custom-call(bf16[128,2048]{1,0:T(8,128)(2,1)} %get-tuple-element.9.att_in, f32[32,128]{1,0:T(8,128)} %get-tuple-element.10.lse_in, f32[1,128]{1,0:T(1,128)} %get-tuple-element.11.tw_in), custom_call_target="tpu_custom_call" | custom-call | tf_op jit(solution)/shard_map/store_results/pallas_call | solution.py:535

commit v4 on v3

--- a/solution.py
+++ b/solution.py
@@ -21,8 +21,9 @@
 BF16 = jnp.bfloat16
 NT = (((1,), (1,)), ((), ()))
 Q_CHUNK = 512
-HEADS_STEP = 4
-DOC_AT = 2
+HEADS_STEP = 8
+DOC_AT = 3
+HOOK_0, HOOK_1, HOOK_2 = 2, 2, 0
 
 
 def iota(shape, dim):
@@ -141,12 +142,16 @@
     chips = back // 2
     z = lax.rem(me // 2, chips)
     corner = me - 2 * z
-    bufs = (vbuf, kbuf)
+    pieces_v, pieces_k = (0, 1), (2, 3)
+
+    def piece(t, slot):
+        if t < 2:
+            return vbuf.at[slot, pl.ds(t * (kv_heads // 2), kv_heads // 2)]
+        return kbuf.at[slot, t - 2]
 
     def slot_copy(t, src, dst, sem, device):
-        buf = bufs[t]
         return pltpu.make_async_remote_copy(
-            src_ref=buf.at[src], dst_ref=buf.at[dst], send_sem=kv_ssem.at[t, sem],
+            src_ref=piece(t, src), dst_ref=piece(t, dst), send_sem=kv_ssem.at[t, sem],
             recv_sem=kv_rsem.at[t, dst], device_id={"cp": device}, device_id_type=MESH,
         )
 
@@ -157,7 +162,7 @@
         return slot_copy(t, back, 0, 0, ahead(back))
 
     def partner_copy(t, src, dst):
-        return slot_copy(t, src, dst, chips + src // 2 if src != back else chips, me + 1 - 2 * core)
+        return slot_copy(t, src, dst, chips + (src // 2) % chips, me + 1 - 2 * core)
 
     def send_own(t):
         @pl.when(core == 0)
@@ -165,18 +170,20 @@
             partner_copy(t, back, back - 1).start()
 
         next_row_copy(t).start()
-        for k in range(1, chips):
+        for k in (3, 1):
             @pl.when(z + k < chips)
             def _(k=k):
                 row_copy(t, k, back).start()
 
+        slot_copy(t, back, back // 2, 2, ahead(back // 2)).start()
+
     def arrived(t, slot):
         slot_copy(t, slot, slot, 0, me).wait_recv()
 
     def serve(t, slot):
         arrived(t, slot)
-        if slot == 0:
-            for k in range(1, chips):
+        if isinstance(slot, int) and slot == 0:
+            for k in (3, 1):
                 @pl.when(z + k >= chips)
                 def _(k=k):
                     row_copy(t, k, 0).start()
@@ -204,7 +211,8 @@
             at = i * Q_CHUNK + t * 128
             qt[at:at + 128] = part[:, t * 128:(t + 1) * 128].T
 
-    send_own(0)
+    for t in pieces_v:
+        send_own(t)
 
     def docs_all():
         part = docs_buf.at[pl.ds(0, back)]
@@ -249,12 +257,14 @@
         u = raw_kt[t]
         u = jnp.concatenate([rope(u[:HEAD_DIM]), rope(u[HEAD_DIM:])], axis=0)
         kbuf[back, t] = u.T.astype(BF16)
-    send_own(1)
-
+    for t in pieces_k:
+        send_own(t)
+
+    for t in pieces_v:
+        serve(t, 0)
     for i in range(DOC_AT, n_chunks):
         q_part(i)
 
-    serve(0, 0)
     scale = HEAD_DIM ** (-0.5)
     zeros = jnp.zeros((HEAD_DIM, rows), BF16)
     for h in range(heads):
@@ -271,33 +281,52 @@
             allowed = allowed & (sub <= lane)
         bias[b] = jnp.where(allowed, 0.0, MASKED)
 
-    serve(1, 0)
     extra = 1 + 6 * core
-    odds = tuple(b + 1 - 2 * core for b in (6, 4, 2))
-
-    def before_0():
-        arrived(0, extra)
-        arrived(1, extra)
-
-    def before_1():
-        for slot in (6, 4, 2):
-            serve(0, slot)
-            serve(1, slot)
-
-    def before_2():
-        for slot in odds:
-            arrived(0, slot)
-            arrived(1, slot)
+    front = (3 - z) // 3
+    one = 6 - 2 * front
+    three = 2 + 4 * front
+    two_ = 12 - one - three
+
+    def odd(slot):
+        return slot + 1 - 2 * core
+
+    def serve_all(slot):
+        for t in pieces_v + pieces_k:
+            serve(t, slot)
+
+    def wait_all(slot):
+        for t in pieces_v + pieces_k:
+            arrived(t, slot)
+
+    def serve_next_row():
+        for t in pieces_k:
+            serve(t, 0)
+
+    def before_first():
+        serve_next_row()
+
+        @pl.when(z > 0)
+        def _():
+            serve_all(one)
+
+        wait_all(extra)
+
+    def serve_first():
+        @pl.when(z == 0)
+        def _():
+            serve_all(one)
 
     groups = (
-        (before_0, (back, 0, extra)),
-        (before_1, (6, 4, 2)),
-        (before_2, odds),
+        ((back,), lambda: None, -1, None),
+        ((0, extra), before_first, HOOK_0, serve_first),
+        ((one, odd(one)), lambda: wait_all(odd(one)), HOOK_1, lambda: serve_all(two_)),
+        ((two_, odd(two_)), lambda: wait_all(odd(two_)), HOOK_2, lambda: serve_all(three)),
+        ((three, odd(three)), lambda: wait_all(odd(three)), -1, None),
     )
     two = HEADS_STEP * rows
     head_lane = iota((1, two), 1) // rows
     acc_rows = HEAD_DIM + 16
-    for gi, (before, slots) in enumerate(groups):
+    for gi, (slots, before, hook_at, hook) in enumerate(groups):
         with jax.named_scope("before%d" % gi):
             before()
         first, last = gi == 0, gi == len(groups) - 1
@@ -362,6 +391,9 @@
         with jax.named_scope("loop%d" % gi):
             score(0, s_even, top_even)
             for j in range(0, pairs, 2):
+                if j == hook_at:
+                    with jax.named_scope("hook%d" % gi):
+                        hook()
                 score(j + 1, s_odd, top_odd)
                 mix(j, s_even, top_even)
                 if j + 2 < pairs:
@@ -434,7 +466,7 @@
     for c in sends:
         c.wait_send()
     docs_all().wait_send()
-    for t in range(2):
+    for t in range(4):
         for sem in range(2 * chips):
             slot_copy(t, back, 0, sem, me).wait_send()
     lse_all().wait_send()
@@ -472,7 +504,7 @@
         back = DOC_MOST // rows
         slots = back + 1
         pairs = heads // HEADS_STEP
-        widest = 3 * rows
+        widest = 2 * rows
         shape = (rows, width, heads, kv_heads, shards, dps)
         hbm = pl.BlockSpec(memory_space=pltpu.HBM)
         dma = pltpu.SemaphoreType.DMA
@@ -519,7 +551,7 @@
                 pltpu.VMEM((1, rows), F32),
                 dma((8,)), dma((qdim // Q_CHUNK,)),
                 dma((2,)),
-                dma((2, back)), dma((2, back)),
+                dma((4, back)), dma((4, back)),
                 dma((dps - 1,)), dma((dps - 1,)),
                 dma((2,)),
             ],

time: 33 us -> 31.4 us (0.952)
  Pallas kernels: 32.3 us -> 30.6 us
    pallas_call x1, Pallas kernels: 30.4 us -> 28.7 us  [body(): pl.pallas_call(functools.partial(kernel, shape), name='attention_step', o...]
where the time goes in v4:
time: 31.4 us; the launch traced here: 31.2 us
  Pallas kernels  30.6 us (97%)
  between operations  0.64 us (2%)
    pallas_call x1, Pallas kernels, body(): pl.pallas_call(functools.partial(kernel, shape), name='attention_step', o...  28.7 us
    pallas_call x1, Pallas kernels, body(): pl.pallas_call(store, name='store_results', out_shape=tuple((jax.ShapeDty...  1.86 us

profile of v4, /device:TPU:1, one launch (start us, length us, event | category | flops | bytes accessed | tf_op | source)
XLA Modules:
  0.0 31.2 jit_solution(477349608703172857)
XLA Ops:
  0.6 28.7 %attention_step.1 = (bf16[128,2048]{1,0:T(8,128)(2,1)}, f32[32,128]{1,0:T(8,128)}, f32[1,128]{1,0:T(1,128)}) custom-call(bf16[2880,128]{1,0:T(8,128)(2,1)} %bitcast.6, f32[2880]{0:T(1024)} %gain_hbm.1, bf16[2880,2048]{1,0:T(8,128)(2,1)} %qw_hbm.1, bf16[2880,512]{1,0:T(8,128)(2,1)} %kvw_hbm.1, f32[32]{0:T(128)} %sink_hbm.1, s32[1,128]{1,0:T(1,128)} %docs_hbm.1, ...), custom_call_target="tpu_custom_call" | custom-call | tf_op jit(solution)/shard_map/attention_step/pallas_call | solution.py:511
  29.4 1.9 %store_results.1 = (bf16[128,2048]{1,0:T(8,128)(2,1)}, f32[32,128]{1,0:T(8,128)}, f32[1,128]{1,0:T(1,128)}) custom-call(bf16[128,2048]{1,0:T(8,128)(2,1)} %get-tuple-element.9.att_in, f32[32,128]{1,0:T(8,128)} %get-tuple-element.10.lse_in, f32[1,128]{1,0:T(1,128)} %get-tuple-element.11.tw_in), custom_call_target="tpu_custom_call" | custom-call | tf_op jit(solution)/shard_map/store_results/pallas_call | solution.py:567

commit v5 on v4

--- a/solution.py
+++ b/solution.py
@@ -23,7 +23,7 @@
 Q_CHUNK = 512
 HEADS_STEP = 8
 DOC_AT = 3
-HOOK_0, HOOK_1, HOOK_2 = 2, 2, 0
+HOOK_0, HOOK_1 = 2, 2
 
 
 def iota(shape, dim):
@@ -170,10 +170,18 @@
             partner_copy(t, back, back - 1).start()
 
         next_row_copy(t).start()
-        for k in (3, 1):
-            @pl.when(z + k < chips)
-            def _(k=k):
-                row_copy(t, k, back).start()
+        @pl.when(z == 0)
+        def _():
+            row_copy(t, 3, back).start()
+
+        @pl.when(z < chips - 1)
+        def _():
+            row_copy(t, 1, back).start()
+
+    def send_two(t):
+        @pl.when(z == 1)
+        def _():
+            slot_copy(t, back, back - 6, 3, ahead(6)).start()
 
         slot_copy(t, back, back // 2, 2, ahead(back // 2)).start()
 
@@ -183,10 +191,13 @@
     def serve(t, slot):
         arrived(t, slot)
         if isinstance(slot, int) and slot == 0:
-            for k in (3, 1):
-                @pl.when(z + k >= chips)
-                def _(k=k):
-                    row_copy(t, k, 0).start()
+            @pl.when(z > 1)
+            def _():
+                row_copy(t, 3, 0).start()
+
+            @pl.when(z == chips - 1)
+            def _():
+                row_copy(t, 1, 0).start()
 
             @pl.when(core == 1)
             def _():
@@ -213,6 +224,8 @@
 
     for t in pieces_v:
         send_own(t)
+    for t in pieces_v:
+        send_two(t)
 
     def docs_all():
         part = docs_buf.at[pl.ds(0, back)]
@@ -233,12 +246,12 @@
     chosen = chosen.astype(F32).astype(BF16)
     chosen3[...] = jnp.concatenate([chosen] * 3, axis=1)
 
-    docs_all().wait_recv()
     square = (rows, 128)
     lane = iota(square, 1)
     sub = iota(square, 0)
-    own_row = jnp.broadcast_to(own_docs.astype(F32), square)
-    own_col = own_row.T
+    own_col = jnp.broadcast_to(own_docs.astype(F32), square).T
+
+    docs_all().wait_recv()
     count = jnp.zeros(square, F32)
     for b in range(back + 1):
         window_docs = docs_buf[b].astype(F32)
@@ -259,6 +272,8 @@
         kbuf[back, t] = u.T.astype(BF16)
     for t in pieces_k:
         send_own(t)
+    for t in pieces_k:
+        send_two(t)
 
     for t in pieces_v:
         serve(t, 0)
@@ -283,7 +298,7 @@
 
     extra = 1 + 6 * core
     front = (3 - z) // 3
-    one = 6 - 2 * front
+    one = 6 - 4 * front
     three = 2 + 4 * front
     two_ = 12 - one - three
 
@@ -305,22 +320,26 @@
     def before_first():
         serve_next_row()
 
-        @pl.when(z > 0)
+        @pl.when(z > 1)
         def _():
             serve_all(one)
 
         wait_all(extra)
 
     def serve_first():
-        @pl.when(z == 0)
+        @pl.when(z <= 1)
         def _():
             serve_all(one)
+
+    def odd_pair():
+        wait_all(odd(one))
+        wait_all(odd(two_))
 
     groups = (
         ((back,), lambda: None, -1, None),
         ((0, extra), before_first, HOOK_0, serve_first),
-        ((one, odd(one)), lambda: wait_all(odd(one)), HOOK_1, lambda: serve_all(two_)),
-        ((two_, odd(two_)), lambda: wait_all(odd(two_)), HOOK_2, lambda: serve_all(three)),
+        ((one, two_), lambda: serve_all(two_), HOOK_1, lambda: serve_all(three)),
+        ((odd(one), odd(two_)), odd_pair, -1, None),
         ((three, odd(three)), lambda: wait_all(odd(three)), -1, None),
     )
     two = HEADS_STEP * rows

time: 31.4 us -> 30.6 us (0.975)
  Pallas kernels: 30.6 us -> 29.8 us
    pallas_call x1, Pallas kernels: 28.7 us -> 28 us  [body(): pl.pallas_call(functools.partial(kernel, shape), name='attention_step', o...]
where the time goes in v5:
time: 30.6 us; the launch traced here: 30.5 us
  Pallas kernels  29.8 us (97%)
  between operations  0.64 us (2%)
    pallas_call x1, Pallas kernels, body(): pl.pallas_call(functools.partial(kernel, shape), name='attention_step', o...  28 us
    pallas_call x1, Pallas kernels, body(): pl.pallas_call(store, name='store_results', out_shape=tuple((jax.ShapeDty...  1.86 us

profile of v5, /device:TPU:1, one launch (start us, length us, event | category | flops | bytes accessed | tf_op | source)
XLA Modules:
  0.0 30.5 jit_solution(11283806127885994837)
XLA Ops:
  0.6 28.0 %attention_step.1 = (bf16[128,2048]{1,0:T(8,128)(2,1)}, f32[32,128]{1,0:T(8,128)}, f32[1,128]{1,0:T(1,128)}) custom-call(bf16[2880,128]{1,0:T(8,128)(2,1)} %bitcast.6, f32[2880]{0:T(1024)} %gain_hbm.1, bf16[2880,2048]{1,0:T(8,128)(2,1)} %qw_hbm.1, bf16[2880,512]{1,0:T(8,128)(2,1)} %kvw_hbm.1, f32[32]{0:T(128)} %sink_hbm.1, s32[1,128]{1,0:T(1,128)} %docs_hbm.1, ...), custom_call_target="tpu_custom_call" | custom-call | tf_op jit(solution)/shard_map/attention_step/pallas_call | solution.py:530
  28.6 1.9 %store_results.1 = (bf16[128,2048]{1,0:T(8,128)(2,1)}, f32[32,128]{1,0:T(8,128)}, f32[1,128]{1,0:T(1,128)}) custom-call(bf16[128,2048]{1,0:T(8,128)(2,1)} %get-tuple-element.9.att_in, f32[32,128]{1,0:T(8,128)} %get-tuple-element.10.lse_in, f32[1,128]{1,0:T(1,128)} %get-tuple-element.11.tw_in), custom_call_target="tpu_custom_call" | custom-call | tf_op jit(solution)/shard_map/store_results/pallas_call | solution.py:586

commit v6 on v5

--- a/solution.py
+++ b/solution.py
@@ -149,20 +149,29 @@
             return vbuf.at[slot, pl.ds(t * (kv_heads // 2), kv_heads // 2)]
         return kbuf.at[slot, t - 2]
 
-    def slot_copy(t, src, dst, sem, device):
+    def whole(kind, part):
+        buf = (vbuf, kbuf)[kind].at[part]
         return pltpu.make_async_remote_copy(
-            src_ref=piece(t, src), dst_ref=piece(t, dst), send_sem=kv_ssem.at[t, sem],
-            recv_sem=kv_rsem.at[t, dst], device_id={"cp": device}, device_id_type=MESH,
+            src_ref=buf, dst_ref=buf, send_sem=kv_ssem.at[kind],
+            recv_sem=kv_rsem.at[kind, 0 if isinstance(part, slice) else part],
+            device_id={"cp": me}, device_id_type=MESH,
         )
 
+    def slot_copy(t, src, dst, device):
+        second = isinstance(dst, int) and dst == 0 and t % 2 == 1
+        return pltpu.make_async_remote_copy(
+            src_ref=piece(t, src), dst_ref=piece(t, dst), send_sem=kv_ssem.at[t // 2],
+            recv_sem=kv_rsem.at[t // 2, back if second else dst], device_id={"cp": device}, device_id_type=MESH,
+        )
+
     def row_copy(t, k, src):
-        return slot_copy(t, src, back - 2 * k, k, corner + 2 * lax.rem(z + k, chips))
+        return slot_copy(t, src, back - 2 * k, corner + 2 * lax.rem(z + k, chips))
 
     def next_row_copy(t):
-        return slot_copy(t, back, 0, 0, ahead(back))
+        return slot_copy(t, back, 0, ahead(back))
 
     def partner_copy(t, src, dst):
-        return slot_copy(t, src, dst, chips + (src // 2) % chips, me + 1 - 2 * core)
+        return slot_copy(t, src, dst, me + 1 - 2 * core)
 
     def send_own(t):
         @pl.when(core == 0)
@@ -181,29 +190,24 @@
     def send_two(t):
         @pl.when(z == 1)
         def _():
-            slot_copy(t, back, back - 6, 3, ahead(6)).start()
-
-        slot_copy(t, back, back // 2, 2, ahead(back // 2)).start()
-
-    def arrived(t, slot):
-        slot_copy(t, slot, slot, 0, me).wait_recv()
-
-    def serve(t, slot):
-        arrived(t, slot)
-        if isinstance(slot, int) and slot == 0:
-            @pl.when(z > 1)
-            def _():
-                row_copy(t, 3, 0).start()
-
-            @pl.when(z == chips - 1)
-            def _():
-                row_copy(t, 1, 0).start()
-
-            @pl.when(core == 1)
-            def _():
-                partner_copy(t, 0, 1).start()
-        else:
-            partner_copy(t, slot, slot - 1 + 2 * core).start()
+            slot_copy(t, back, back - 6, ahead(6)).start()
+
+        slot_copy(t, back, back // 2, ahead(back // 2)).start()
+
+    def serve(t):
+        slot_copy(t, 0, 0, me).wait_recv()
+
+        @pl.when(z > 1)
+        def _():
+            row_copy(t, 3, 0).start()
+
+        @pl.when(z == chips - 1)
+        def _():
+            row_copy(t, 1, 0).start()
+
+        @pl.when(core == 1)
+        def _():
+            partner_copy(t, 0, 1).start()
 
     loads[4].wait()
     kv = jnp.dot(normed[...], kvw[...], preferred_element_type=F32)
@@ -276,7 +280,7 @@
         send_two(t)
 
     for t in pieces_v:
-        serve(t, 0)
+        serve(t)
     for i in range(DOC_AT, n_chunks):
         q_part(i)
 
@@ -306,16 +310,18 @@
         return slot + 1 - 2 * core
 
     def serve_all(slot):
-        for t in pieces_v + pieces_k:
-            serve(t, slot)
+        for kind in range(2):
+            whole(kind, slot).wait_recv()
+            for t in (2 * kind, 2 * kind + 1):
+                partner_copy(t, slot, slot - 1 + 2 * core).start()
 
     def wait_all(slot):
-        for t in pieces_v + pieces_k:
-            arrived(t, slot)
+        for kind in range(2):
+            whole(kind, slot).wait_recv()
 
     def serve_next_row():
         for t in pieces_k:
-            serve(t, 0)
+            serve(t)
 
     def before_first():
         serve_next_row()
@@ -485,9 +491,8 @@
     for c in sends:
         c.wait_send()
     docs_all().wait_send()
-    for t in range(4):
-        for sem in range(2 * chips):
-            slot_copy(t, back, 0, sem, me).wait_send()
+    for kind in range(2):
+        whole(kind, slice(0, back)).wait_send()
     lse_all().wait_send()
     att_copy.wait()
     tw_move.wait()
@@ -570,7 +575,7 @@
                 pltpu.VMEM((1, rows), F32),
                 dma((8,)), dma((qdim // Q_CHUNK,)),
                 dma((2,)),
-                dma((4, back)), dma((4, back)),
+                dma((2,)), dma((2, back + 1)),
                 dma((dps - 1,)), dma((dps - 1,)),
                 dma((2,)),
             ],

time: 30.6 us -> 30.2 us (0.987)
  Pallas kernels: 29.8 us -> 29.4 us
    pallas_call x1, Pallas kernels: 28 us -> 27.6 us  [body(): pl.pallas_call(functools.partial(kernel, shape), name='attention_step', o...]
where the time goes in v6:
time: 30.2 us; the launch traced here: 30.1 us
  Pallas kernels  29.4 us (97%)
  between operations  0.64 us (2%)
    pallas_call x1, Pallas kernels, body(): pl.pallas_call(functools.partial(kernel, shape), name='attention_step', o...  27.6 us
    pallas_call x1, Pallas kernels, body(): pl.pallas_call(store, name='store_results', out_shape=tuple((jax.ShapeDty...  1.86 us

profile of v6, /device:TPU:1, one launch (start us, length us, event | category | flops | bytes accessed | tf_op | source)
XLA Modules:
  0.0 30.1 jit_solution(8424601927440593328)
XLA Ops:
  0.6 27.6 %attention_step.1 = (bf16[128,2048]{1,0:T(8,128)(2,1)}, f32[32,128]{1,0:T(8,128)}, f32[1,128]{1,0:T(1,128)}) custom-call(bf16[2880,128]{1,0:T(8,128)(2,1)} %bitcast.6, f32[2880]{0:T(1024)} %gain_hbm.1, bf16[2880,2048]{1,0:T(8,128)(2,1)} %qw_hbm.1, bf16[2880,512]{1,0:T(8,128)(2,1)} %kvw_hbm.1, f32[32]{0:T(128)} %sink_hbm.1, s32[1,128]{1,0:T(1,128)} %docs_hbm.1, ...), custom_call_target="tpu_custom_call" | custom-call | tf_op jit(solution)/shard_map/attention_step/pallas_call | solution.py:535
  28.2 1.9 %store_results.1 = (bf16[128,2048]{1,0:T(8,128)(2,1)}, f32[32,128]{1,0:T(8,128)}, f32[1,128]{1,0:T(1,128)}) custom-call(bf16[128,2048]{1,0:T(8,128)(2,1)} %get-tuple-element.9.att_in, f32[32,128]{1,0:T(8,128)} %get-tuple-element.10.lse_in, f32[1,128]{1,0:T(1,128)} %get-tuple-element.11.tw_in), custom_call_target="tpu_custom_call" | custom-call | tf_op jit(solution)/shard_map/store_results/pallas_call | solution.py:591
